TPU v7x, 32 devices: a whole 2x2x4 slice. The times are simulated.
32 devices in a mesh: dp: 4 (over y, x), mp: 8 (over z, core).
Axes of the slice: x: 2, y: 2, z: 4, core: 2. Of those that a mesh axis runs over, the one named last changes fastest.
Arguments:
- query_grads: bfloat16 [4, 1, 3584, 4096], P('dp', None, None, 'mp'), may hold values from -102 to 102
- merge_grads: bfloat16 [4, 1, 4096, 3584], P('dp', None, 'mp'), may hold values from -102 to 102
- query_accum: float32 [1, 3584, 4096], P(None, 'dp', 'mp'), may hold values from -406 to 406
- merge_accum: float32 [1, 4096, 3584], P(None, 'mp', 'dp'), may hold values from -406 to 406
- query_master: float32 [1, 3584, 4096], P(None, 'dp', 'mp'), may hold values from -0.75 to 0.75
- merge_master: float32 [1, 4096, 3584], P(None, 'mp', 'dp'), may hold values from -0.75 to 0.75
- query_moment: float32 [1, 3584, 4096], P(None, 'dp', 'mp'), may hold values from -6 to 6
- merge_moment: float32 [1, 4096, 3584], P(None, 'mp', 'dp'), may hold values from -6 to 6
- query_second: float32 [1, 3584, 4096], P(None, 'dp', 'mp'), may hold values from 0.3 to 3
- merge_second: float32 [1, 4096, 3584], P(None, 'mp', 'dp'), may hold values from 0.3 to 3
Outputs:
- query_weight: bfloat16 [1, 3584, 4096], P(None, None, 'mp')
- merge_weight: bfloat16 [1, 4096, 3584], P(None, 'mp')
- query_shard: float32 [1, 3584, 4096], P(None, 'dp', 'mp')
- merge_shard: float32 [1, 4096, 3584], P(None, 'mp', 'dp')
- query_first: float32 [1, 3584, 4096], P(None, 'dp', 'mp')
- merge_first: float32 [1, 4096, 3584], P(None, 'mp', 'dp')
- query_variance: float32 [1, 3584, 4096], P(None, 'dp', 'mp')
- merge_variance: float32 [1, 4096, 3584], P(None, 'mp', 'dp')
All inputs are finite; a program needn't handle non-finite values.
Results may differ from a plain program's by a relative error of at most 0.0015.
Values may be sent and summed in bfloat16 or wider, within the bound.
No kernel may reach another device: no remote copies, remote signals or barrier semaphores. Data moves between devices by JAX's collectives and lax.ppermute only.
A program may use at most 128 MiB of HBM per device.

v0:
```python
import functools

import jax
import jax.numpy as jnp
from jax import lax
from jax.experimental import pallas as pl
from jax.experimental.pallas import tpu as pltpu
from jax.sharding import PartitionSpec as P


STEP = 10

beta_one = 0.9
beta_two = 0.95
learn_rate = 0.002
weight_decay = 0.1
adam_eps = 1e-08

BLOCKS = 4
HEAD = 1


def adamw(total, clip, master, moment, second):
    scaled = clip * total
    first = beta_one * moment + (1.0 - beta_one) * scaled
    variance = beta_two * second + (1.0 - beta_two) * scaled * scaled
    corr_one = 1.0 - beta_one**STEP
    corr_two = 1.0 - beta_two**STEP
    update = first * (1.0 / corr_one) / (jnp.sqrt(variance * (1.0 / corr_two)) + adam_eps)
    return (master - learn_rate * (update + weight_decay * master), first, variance)


class Layout:
    def __init__(self, rows, cols, axis, parts):
        self.rows, self.cols, self.axis, self.parts = rows, cols, axis, parts
        self.step = rows // BLOCKS
        self.block = (self.step, cols)
        self.whole = (rows * parts, cols) if axis == 0 else (rows, cols * parts)

    def piece(self, partner, start=0):
        def index(i):
            owner = lax.axis_index("dp") ^ partner
            return (owner * BLOCKS + start + i, 0) if self.axis == 0 else (start + i, owner)

        return pl.BlockSpec(self.block, index)

    def shard(self, start=0):
        return pl.BlockSpec(self.block, lambda i: (start + i, 0))

    def short(self):
        return pl.BlockSpec(self.block, lambda i: (jnp.minimum(i, HEAD - 1), 0))

    def long(self):
        return pl.BlockSpec(self.block, lambda i: (jnp.maximum(i - HEAD, 0), 0))

    def array(self, blocks, dtype):
        return jax.ShapeDtypeStruct((blocks * self.step, self.cols), dtype)

    def bytes(self, blocks, width):
        return blocks * self.step * self.cols * width


def call(body, grid, in_specs, out_specs, out_shape, cost, aliases=None):
    return pl.pallas_call(
        body,
        grid=(grid,),
        in_specs=in_specs,
        out_specs=out_specs,
        out_shape=out_shape,
        input_output_aliases=aliases or {},
        compiler_params=pltpu.CompilerParams(
            dimension_semantics=("arbitrary",), vmem_limit_bytes=24 * 2**20
        ),
        cost_estimate=pl.CostEstimate(flops=cost * 2, bytes_accessed=cost, transcendentals=0),
    )


def copy_body(source, target):
    target[...] = source[...]


def extract(lay, grads, partner):
    return call(
        copy_body, BLOCKS, [lay.piece(partner)], lay.shard(), lay.array(BLOCKS, jnp.bfloat16), lay.bytes(BLOCKS, 4)
    )(grads)


def add_body(grads, arrived, short, long):
    value = (grads[...].astype(jnp.float32) + arrived[...].astype(jnp.float32)).astype(jnp.bfloat16)
    i = pl.program_id(0)

    @pl.when(i < HEAD)
    def _():
        short[...] = value

    @pl.when(i >= HEAD)
    def _():
        long[...] = value


def add_forward(lay, grads, arrived, partner):
    return call(
        add_body,
        BLOCKS,
        [lay.piece(partner), lay.shard()],
        [lay.short(), lay.long()],
        [lay.array(HEAD, jnp.bfloat16), lay.array(BLOCKS - HEAD, jnp.bfloat16)],
        lay.bytes(BLOCKS, 6),
    )(grads, arrived)


def partial_body(grads, arrived, accum, out):
    out[...] = accum[...] + (grads[...].astype(jnp.float32) + arrived[...].astype(jnp.float32))


def partial_sum(lay, grads, arrived, accum):
    return call(
        partial_body,
        BLOCKS,
        [lay.piece(0), lay.shard(), lay.shard()],
        lay.shard(),
        lay.array(BLOCKS, jnp.float32),
        lay.bytes(BLOCKS, 12),
    )(grads, arrived, accum)


def squares(held, arrived):
    total = held[...] + arrived[...].astype(jnp.float32)
    rows, cols = total.shape
    tile = jnp.sum((total * total).reshape(rows // 8, 8, cols), axis=0)
    return sum(tile[:, k : k + 128] for k in range(0, cols, 128))


def long_body(held, arrived, out):
    @pl.when(pl.program_id(0) == 0)
    def _():
        out[...] = jnp.zeros_like(out)

    out[...] += squares(held, arrived)


def long_squares(lay, held, arrived):
    n = BLOCKS - HEAD
    return call(
        long_body,
        n,
        [lay.shard(HEAD), lay.shard()],
        pl.BlockSpec((8, 128), lambda i: (0, 0)),
        jax.ShapeDtypeStruct((8, 128), jnp.float32),
        lay.bytes(n, 6),
    )(held, arrived)


def short_body(held_one, arrived_one, held_two, arrived_two, sum_one, sum_two, out):
    value = squares(held_one, arrived_one) + squares(held_two, arrived_two)

    @pl.when(pl.program_id(0) == 0)
    def _():
        out[...] = jnp.broadcast_to(jnp.sum(sum_one[...] + sum_two[...], axis=0, keepdims=True), out.shape)

    out[...] += jnp.broadcast_to(jnp.sum(value, axis=0, keepdims=True), out.shape)


def short_squares(lays, helds, arriveds, sums, devices):
    tile = pl.BlockSpec((8, 128), lambda i: (0, 0))
    one, two = lays
    return call(
        short_body,
        HEAD,
        [one.shard(), one.shard(), two.shard(), two.shard(), tile, tile],
        pl.BlockSpec((devices, 128), lambda i: (0, 0)),
        jax.ShapeDtypeStruct((devices, 128), jnp.float32),
        one.bytes(HEAD, 12),
    )(helds[0], arriveds[0], helds[1], arriveds[1], *sums)


def clip_of(entries, sums):
    sumsq = jnp.sum(jnp.sum(sums[...], axis=0, keepdims=True), axis=1, keepdims=True)
    return jnp.minimum(1.0, lax.rsqrt(sumsq / entries + 1e-06))


def weight_body(entries, sums, held, arrived, master, moment, second, out):
    total = held[...] + arrived[...].astype(jnp.float32)
    shard, _, _ = adamw(total, clip_of(entries, sums), master[...], moment[...], second[...])
    out[...] = shard.astype(jnp.bfloat16)


def weight_piece(lay, start, blocks, entries, sums, held, arrived, state):
    return call(
        functools.partial(weight_body, entries),
        blocks,
        [pl.BlockSpec(sums.shape, lambda i: (0, 0)), lay.shard(start), lay.shard()] + [lay.shard(start)] * 3,
        lay.shard(),
        lay.array(blocks, jnp.bfloat16),
        lay.bytes(blocks, 20),
    )(sums, held, arrived, *state)


def update_body(entries, sums, held, short, long, master, moment, second, shard_out, first_out, variance_out):
    arrived = jnp.where(
        pl.program_id(0) < HEAD, short[...].astype(jnp.float32), long[...].astype(jnp.float32)
    )
    shard, first, variance = adamw(
        held[...] + arrived, clip_of(entries, sums), master[...], moment[...], second[...]
    )
    shard_out[...] = shard
    first_out[...] = first
    variance_out[...] = variance


def update(lay, entries, sums, held, short, long, state):
    return call(
        functools.partial(update_body, entries),
        BLOCKS,
        [pl.BlockSpec(sums.shape, lambda i: (0, 0)), lay.shard(), lay.short(), lay.long()] + [lay.shard()] * 3,
        [lay.shard()] * 3,
        [lay.array(BLOCKS, jnp.float32)] * 3,
        lay.bytes(BLOCKS, 30),
    )(sums, held, short, long, *state)


def place_body(*refs):
    short, long, out = refs[-3:]
    out[...] = jnp.where(pl.program_id(0) < HEAD, short[...], long[...])


def place(lay, whole, short, long, partner):
    first = whole is None
    return call(
        place_body,
        BLOCKS,
        ([] if first else [pl.BlockSpec(memory_space=pl.ANY)]) + [lay.short(), lay.long()],
        lay.piece(partner),
        jax.ShapeDtypeStruct(lay.whole, jnp.bfloat16),
        lay.bytes(BLOCKS, 4),
        aliases=None if first else {0: 0},
    )(*([] if first else [whole]), short, long)


def place_long_body(_, long, out):
    out[...] = long[...]


def place_long(lay, whole, long, partner):
    return call(
        place_long_body,
        BLOCKS - HEAD,
        [pl.BlockSpec(memory_space=pl.ANY), lay.shard()],
        lay.piece(partner, HEAD),
        jax.ShapeDtypeStruct(lay.whole, jnp.bfloat16),
        lay.bytes(BLOCKS - HEAD, 4),
        aliases={0: 0},
    )(whole, long)


def place_short_body(_, __, one, two, out_one, out_two):
    out_one[...] = one[...]
    out_two[...] = two[...]


def place_short(lays, wholes, shorts, partner):
    one, two = lays
    hbm = pl.BlockSpec(memory_space=pl.ANY)
    return call(
        place_short_body,
        HEAD,
        [hbm, hbm, one.shard(), two.shard()],
        [one.piece(partner), two.piece(partner)],
        [jax.ShapeDtypeStruct(lay.whole, jnp.bfloat16) for lay in lays],
        one.bytes(HEAD, 8),
        aliases={0: 0, 1: 1},
    )(*wholes, *shorts)


def exchange(value, partner, parts):
    return lax.ppermute(value, "dp", [(i, i ^ partner) for i in range(parts)])


def on_square(parts, devices, entries, *args):
    grads = [a.reshape(a.shape[-2:]) for a in args[:2]]
    accums = [a.reshape(a.shape[-2:]) for a in args[2:4]]
    states = [[a.reshape(a.shape[-2:]) for a in args[4 + k :: 2]] for k in range(2)]
    lays = [Layout(*accums[k].shape, k, parts) for k in range(2)]
    near, far = (1, 2), (2, 1)
    both = range(2)

    def step(function, *lists):
        return [function(lays[k], *(x[k] for x in lists)) for k in both]

    def move(values, partners):
        return [exchange(values[k], partners[k], parts) for k in both]

    relayed = move(step(extract, grads, (3, 3)), near)
    direct = move(step(extract, grads, near), near)
    sent = step(add_forward, grads, relayed, far)
    tail = move([x[1] for x in sent], far)
    head = move([x[0] for x in sent], far)
    held = step(partial_sum, grads, direct, accums)
    sums = step(long_squares, held, tail)
    sums = short_squares(lays, held, head, sums, devices)
    sums = lax.all_to_all(sums, ("dp", "mp"), 0, 0, tiled=True)

    def weights(start, blocks):
        return lambda lay, held, arrived, state: weight_piece(lay, start, blocks, entries, sums, held, arrived, state)

    own_head = step(weights(0, HEAD), held, head, states)
    own_tail = step(weights(HEAD, BLOCKS - HEAD), held, tail, states)
    near_head, near_tail = move(own_head, near), move(own_tail, near)
    far_tail, far_head = move(own_tail, far), move(own_head, far)
    last_tail, last_head = move(near_tail, far), move(near_head, far)

    updated = step(lambda lay, *x: update(lay, entries, sums, *x), held, head, tail, states)
    wholes = step(place, (None, None), own_head, own_tail, (0, 0))
    wholes = step(place, wholes, near_head, near_tail, near)
    wholes = step(place, wholes, far_head, far_tail, far)
    wholes = step(place_long, wholes, last_tail, (3, 3))
    wholes = place_short(lays, wholes, last_head, 3)
    return tuple(w[None] for w in wholes) + tuple(updated[k][j][None] for j in range(3) for k in both)


def on_any(entries, *args):
    grads, accums = args[:2], args[2:4]
    states = [args[4 + k :: 2] for k in range(2)]
    axes = (1, 2)
    totals = [
        accums[k]
        + lax.psum_scatter(grads[k][0], "dp", scatter_dimension=axes[k], tiled=True).astype(jnp.float32)
        for k in range(2)
    ]
    sumsq = lax.psum(sum(jnp.sum(t * t) for t in totals), ("dp", "mp"))
    clip = jnp.minimum(1.0, lax.rsqrt(sumsq / entries + 1e-06))
    updated = [adamw(totals[k], clip, *states[k]) for k in range(2)]
    weights = tuple(
        lax.all_gather(updated[k][0].astype(jnp.bfloat16), "dp", axis=axes[k], tiled=True) for k in range(2)
    )
    return weights + tuple(updated[k][j] for j in range(3) for k in range(2))


def solution(mesh):
    parts = mesh.shape["dp"]
    devices = mesh.size

    def on_device(*args):
        entries = float(devices * sum(a.size for a in args[2:4]))
        tiled = all(a.shape[-2] % (16 * BLOCKS) == 0 and a.shape[-1] % 128 == 0 for a in args[2:4])
        if parts == 4 and tiled:
            return on_square(parts, devices, entries, *args)
        return on_any(entries, *args)

    rows, cols = P(None, "dp", "mp"), P(None, "mp", "dp")
    return jax.shard_map(
        on_device,
        mesh=mesh,
        in_specs=(P("dp", None, None, "mp"), P("dp", None, "mp", None)) + (rows, cols) * 4,
        out_specs=(P(None, None, "mp"), P(None, "mp", None)) + (rows, cols) * 3,
        check_vma=False,
    )
```

profile of v0, /device:TPU:0, one launch (start us, length us, event | category | flops | bytes accessed | tf_op | source)
XLA Modules:
  0.0 171.7 jit_solution(1307533130934299824)
XLA Ops:
  0.6 0.0 copy-start
  0.6 2.0 %copy-done = bf16[1,1,3584,512]{3,2,1,0:T(8,128)(2,1)S(1)} copy-done((bf16[1,1,3584,512]{3,2,1,0:T(8,128)(2,1)S(1)}, bf16[1,1,3584,512]{3,2,1,0:T(8,128)(2,1)}, u32[]{:S(2)}) %copy-start) | copy-done | bytes 3670040
  2.7 0.1 shard_map.163
  2.8 3.0 %collective-permute-start.1 = (bf16[896,512]{1,0:T(8,128)(2,1)S(1)}, bf16[896,512]{1,0:T(8,128)(2,1)S(1)}, u32[]{:S(2)}, u32[]{:S(2)}) collective-permute-start(bf16[896,512]{1,0:T(8,128)(2,1)S(1)} %shard_map.163), channel_id=1, source_target_pairs={{0,8},{8,0},{16,24},{24,16},{1,9},{9,1},{17,25},{25,17},{2,10},{10... | collective-permute-start | bytes 2752520 | tf_op jit(solution)/shard_map/ppermute | solution.py:276
  5.9 0.3 shard_map.167
  6.1 1.9 %collective-permute-start.4 = (bf16[512,896]{1,0:T(8,128)(2,1)S(1)}, bf16[512,896]{1,0:T(8,128)(2,1)S(1)}, u32[]{:S(2)}, u32[]{:S(2)}) collective-permute-start(bf16[512,896]{1,0:T(8,128)(2,1)S(1)} %shard_map.167), channel_id=1, source_target_pairs={{0,16},{8,24},{16,0},{24,8},{1,17},{9,25},{17,1},{25,9},{2,18},{10... | collective-permute-start | bytes 2752520 | tf_op jit(solution)/shard_map/ppermute | solution.py:276
  8.1 0.1 shard_map.161
  8.2 1.7 %collective-permute-start = (bf16[896,512]{1,0:T(8,128)(2,1)S(1)}, bf16[896,512]{1,0:T(8,128)(2,1)S(1)}, u32[]{:S(2)}, u32[]{:S(2)}) collective-permute-start(bf16[896,512]{1,0:T(8,128)(2,1)S(1)} %shard_map.161), channel_id=1, source_target_pairs={{0,8},{8,0},{16,24},{24,16},{1,9},{9,1},{17,25},{25,17},{2,10},{10... | collective-permute-start | bytes 2752520 | tf_op jit(solution)/shard_map/ppermute | solution.py:276
  9.9 0.3 shard_map.165
  10.2 1.6 collective-permute-start.3
  11.8 15.3 %collective-permute-done.1.arrived = bf16[896,512]{1,0:T(8,128)(2,1)S(1)} collective-permute-done((bf16[896,512]{1,0:T(8,128)(2,1)S(1)}, bf16[896,512]{1,0:T(8,128)(2,1)S(1)}, u32[]{:S(2)}, u32[]{:S(2)}) %collective-permute-start.1) | collective-permute-done | bytes 917536 | tf_op jit(solution)/shard_map/ppermute | solution.py:276
  27.1 0.5 shard_map.164
  27.5 0.0 copy-start.9
  27.5 2.1 %collective-permute-start.6 = (bf16[672,512]{1,0:T(8,128)(2,1)S(1)}, bf16[672,512]{1,0:T(8,128)(2,1)S(1)}, u32[]{:S(2)}, u32[]{:S(2)}) collective-permute-start(bf16[672,512]{1,0:T(8,128)(2,1)S(1)} %get-tuple-element.22), channel_id=1, source_target_pairs={{0,16},{8,24},{16,0},{24,8},{1,17},{9,25},{17,1},{25,9},{2,18},{10... | collective-permute-start | bytes 2064392 | tf_op jit(solution)/shard_map/ppermute | solution.py:276
  29.7 0.6 shard_map.168
  30.2 1.7 collective-permute-start.7
  31.9 1.5 collective-permute-start.2
  33.4 13.3 %collective-permute-done.arrived = bf16[896,512]{1,0:T(8,128)(2,1)S(1)} collective-permute-done((bf16[896,512]{1,0:T(8,128)(2,1)S(1)}, bf16[896,512]{1,0:T(8,128)(2,1)S(1)}, u32[]{:S(2)}, u32[]{:S(2)}) %collective-permute-start) | collective-permute-done | bytes 917536 | tf_op jit(solution)/shard_map/ppermute | solution.py:276
  46.7 2.0 %collective-permute-start.5 = (bf16[128,896]{1,0:T(8,128)(2,1)S(1)}, bf16[128,896]{1,0:T(8,128)(2,1)S(1)}, u32[]{:S(2)}, u32[]{:S(2)}) collective-permute-start(bf16[128,896]{1,0:T(8,128)(2,1)S(1)} %get-tuple-element.21), channel_id=1, source_target_pairs={{0,8},{8,0},{16,24},{24,16},{1,9},{9,1},{17,25},{25,17},{2,10},{10... | collective-permute-start | bytes 688136 | tf_op jit(solution)/shard_map/ppermute | solution.py:276
  48.7 0.3 shard_map.162.held.held_one
  49.1 0.0 collective-permute-done.3.arrived
  49.1 1.1 copy-done.10
  50.2 0.4 shard_map.166.held.held_two
  50.7 13.2 %collective-permute-done.6.arrived.long = bf16[672,512]{1,0:T(8,128)(2,1)S(1)} collective-permute-done((bf16[672,512]{1,0:T(8,128)(2,1)S(1)}, bf16[672,512]{1,0:T(8,128)(2,1)S(1)}, u32[]{:S(2)}, u32[]{:S(2)}) %collective-permute-start.6) | collective-permute-done | bytes 688160 | tf_op jit(solution)/shard_map/ppermute | solution.py:276
  63.8 0.3 shard_map.169.sum_one
  64.1 0.0 copy-start.8
  64.2 0.3 shard_map.170.sum_two
  64.5 0.0 copy-start.7
  64.5 3.2 %collective-permute-done.2.arrived_one.arrived.short = bf16[224,512]{1,0:T(8,128)(2,1)S(1)} collective-permute-done((bf16[224,512]{1,0:T(8,128)(2,1)S(1)}, bf16[224,512]{1,0:T(8,128)(2,1)S(1)}, u32[]{:S(2)}, u32[]{:S(2)}) %collective-permute-start.2) | collective-permute-done | bytes 229408 | tf_op jit(solution)/shard_map/ppermute | solution.py:276
  67.7 0.2 shard_map.171
  67.9 13.1 %all_to_all.11 = f32[32,1,128]{2,1,0:T(1,128)S(1)} all-to-all(f32[32,1,128]{2,1,0:T(1,128)S(1)} %bitcast.56), channel_id=1, replica_groups=mesh['dp'=4,'mp'=8] {'dp','mp'}, dimensions={0} | all-to-all | bytes 32768 | tf_op jit(solution)/shard_map/all_to_all | solution.py:301
  81.0 0.0 copy-start.3
  81.0 0.0 copy-start.4
  81.0 2.4 %shard_map.179.refs_1_ = bf16[384,896]{1,0:T(8,128)(2,1)S(1)} custom-call(f32[32,128]{1,0:T(8,128)S(1)} %bitcast.50, f32[512,896]{1,0:T(8,128)S(1)} %shard_map.166.held.held_two, bf16[384,896]{1,0:T(8,128)(2,1)S(1)} %collective-permute-done.7.arrived.long, f32[512,896]{1,0:T(8,128)S(1)} %bitcast.39, f32[512,896]{1,0:T(8,128)S(1)} %bitcast.42, ...), custom_call_target="tpu_custom_call" | custom-call | flops 13762560 | bytes 6881280 | tf_op jit(solution)/shard_map/pallas_call | solution.py:189
  83.4 0.7 collective-permute-start.14
  84.1 2.4 %shard_map.173.refs_1_ = bf16[672,512]{1,0:T(8,128)(2,1)S(1)} custom-call(f32[32,128]{1,0:T(8,128)S(1)} %bitcast.51, f32[896,512]{1,0:T(8,128)S(1)} %shard_map.162.held.held_one, bf16[672,512]{1,0:T(8,128)(2,1)S(1)} %collective-permute-done.6.arrived.long, f32[896,512]{1,0:T(8,128)S(1)} %bitcast.30, f32[896,512]{1,0:T(8,128)S(1)} %bitcast.33, ...), custom_call_target="tpu_custom_call" | custom-call | flops 13762560 | bytes 6881280 | tf_op jit(solution)/shard_map/pallas_call | solution.py:189
  86.4 0.6 collective-permute-start.9
  87.1 0.8 shard_map.178.refs_0_
  87.9 1.5 collective-permute-start.13
  89.4 1.4 collective-permute-start.15
  90.8 0.6 collective-permute-start.16
  91.4 14.2 %collective-permute-done.13.refs_1_ = bf16[128,896]{1,0:T(8,128)(2,1)S(1)} collective-permute-done((bf16[128,896]{1,0:T(8,128)(2,1)S(1)}, bf16[128,896]{1,0:T(8,128)(2,1)S(1)}, u32[]{:S(2)}, u32[]{:S(2)}) %collective-permute-start.13) | collective-permute-done | bytes 229408 | tf_op jit(solution)/shard_map/ppermute | solution.py:276
  105.6 0.5 collective-permute-start.11
  106.1 0.6 collective-permute-start.17
  106.7 1.4 collective-permute-start.12
  108.1 0.8 shard_map.172.refs_0_
  108.9 0.9 collective-permute-done.15.refs_1_
  109.7 0.8 collective-permute-start.8
  110.5 32.2 %collective-permute-done.8.refs_1_ = bf16[224,512]{1,0:T(8,128)(2,1)S(1)} collective-permute-done((bf16[224,512]{1,0:T(8,128)(2,1)S(1)}, bf16[224,512]{1,0:T(8,128)(2,1)S(1)}, u32[]{:S(2)}, u32[]{:S(2)}) %collective-permute-start.8) | collective-permute-done | bytes 229408 | tf_op jit(solution)/shard_map/ppermute | solution.py:276
  142.7 1.5 collective-permute-start.10
  144.2 4.7 %collective-permute-done.10.refs_1_ = bf16[224,512]{1,0:T(8,128)(2,1)S(1)} collective-permute-done((bf16[224,512]{1,0:T(8,128)(2,1)S(1)}, bf16[224,512]{1,0:T(8,128)(2,1)S(1)}, u32[]{:S(2)}, u32[]{:S(2)}) %collective-permute-start.10) | collective-permute-done | bytes 229408 | tf_op jit(solution)/shard_map/ppermute | solution.py:276
  148.9 0.6 collective-permute-start.19
  149.5 1.3 collective-permute-start.18
  150.8 1.5 shard_map.180.refs_0_
  152.3 1.5 shard_map.174.refs_0_
  153.8 4.1 %shard_map.185 = (f32[896,512]{1,0:T(8,128)}, f32[896,512]{1,0:T(8,128)}, f32[896,512]{1,0:T(8,128)}) custom-call(f32[32,128]{1,0:T(8,128)S(1)} %bitcast.54, f32[896,512]{1,0:T(8,128)S(1)} %shard_map.162.held.held_one, bf16[224,512]{1,0:T(8,128)(2,1)S(1)} %collective-permute-done.2.arrived_one.arrived.short, ...), custom_call_target="tpu_custom_call" | custom-call | flops 27525120 | bytes 13762560 | tf_op jit(solution)/shard_map/pallas_call | solution.py:212
  157.9 4.1 %shard_map.186 = (f32[512,896]{1,0:T(8,128)}, f32[512,896]{1,0:T(8,128)}, f32[512,896]{1,0:T(8,128)}) custom-call(f32[32,128]{1,0:T(8,128)S(1)} %bitcast.55, f32[512,896]{1,0:T(8,128)S(1)} %shard_map.166.held.held_two, bf16[128,896]{1,0:T(8,128)(2,1)S(1)} %collective-permute-done.5.arrived_two.arrived.short, ...), custom_call_target="tpu_custom_call" | custom-call | flops 27525120 | bytes 13762560 | tf_op jit(solution)/shard_map/pallas_call | solution.py:212
  162.0 1.5 shard_map.181.refs_0_
  163.5 1.5 shard_map.175.refs_0_
  165.0 1.5 shard_map.182._
  166.5 1.5 shard_map.176._
  168.0 1.4 shard_map.183.__
  169.5 1.4 shard_map.177._
  170.9 0.8 shard_map.184
  (25 shorter events, 0.1 us)
Async XLA Ops:
  0.6 2.0 %copy-start = (bf16[1,1,3584,512]{3,2,1,0:T(8,128)(2,1)S(1)}, bf16[1,1,3584,512]{3,2,1,0:T(8,128)(2,1)}, u32[]{:S(2)}) copy-start(bf16[1,1,3584,512]{3,2,1,0:T(8,128)(2,1)} %param.10) | copy-start | bytes 11010052
  2.7 3.2 %copy-start.2 = (bf16[1,1,512,3584]{3,2,1,0:T(8,128)(2,1)S(1)}, bf16[1,1,512,3584]{3,2,1,0:T(8,128)(2,1)}, u32[]{:S(2)}) copy-start(bf16[1,1,512,3584]{3,2,1,0:T(8,128)(2,1)} %param.11) | copy-start | bytes 11010052
  2.8 24.2 %collective-permute-start.1 = (bf16[896,512]{1,0:T(8,128)(2,1)S(1)}, bf16[896,512]{1,0:T(8,128)(2,1)S(1)}, u32[]{:S(2)}, u32[]{:S(2)}) collective-permute-start(bf16[896,512]{1,0:T(8,128)(2,1)S(1)} %shard_map.163), channel_id=1, source_target_pairs={{0,8},{8,0},{16,24},{24,16},{1,9},{9,1},{17,25},{25,17},{2,10},{10... | collective-permute-start | bytes 2752520 | tf_op jit(solution)/shard_map/ppermute | solution.py:276
  5.9 2.2 %copy-start.1 = (bf16[1,1,3584,512]{3,2,1,0:T(8,128)(2,1)S(1)}, bf16[1,1,3584,512]{3,2,1,0:T(8,128)(2,1)}, u32[]{:S(2)}) copy-start(bf16[1,1,3584,512]{3,2,1,0:T(8,128)(2,1)} %param.10) | copy-start | bytes 11010052
  6.1 23.5 %collective-permute-start.4 = (bf16[512,896]{1,0:T(8,128)(2,1)S(1)}, bf16[512,896]{1,0:T(8,128)(2,1)S(1)}, u32[]{:S(2)}, u32[]{:S(2)}) collective-permute-start(bf16[512,896]{1,0:T(8,128)(2,1)S(1)} %shard_map.167), channel_id=1, source_target_pairs={{0,16},{8,24},{16,0},{24,8},{1,17},{9,25},{17,1},{25,9},{2,18},{10... | collective-permute-start | bytes 2752520 | tf_op jit(solution)/shard_map/ppermute | solution.py:276
  8.2 38.5 %collective-permute-start = (bf16[896,512]{1,0:T(8,128)(2,1)S(1)}, bf16[896,512]{1,0:T(8,128)(2,1)S(1)}, u32[]{:S(2)}, u32[]{:S(2)}) collective-permute-start(bf16[896,512]{1,0:T(8,128)(2,1)S(1)} %shard_map.161), channel_id=1, source_target_pairs={{0,8},{8,0},{16,24},{24,16},{1,9},{9,1},{17,25},{25,17},{2,10},{10... | collective-permute-start | bytes 2752520 | tf_op jit(solution)/shard_map/ppermute | solution.py:276
  10.2 38.9 %collective-permute-start.3 = (bf16[512,896]{1,0:T(8,128)(2,1)S(1)}, bf16[512,896]{1,0:T(8,128)(2,1)S(1)}, u32[]{:S(2)}, u32[]{:S(2)}) collective-permute-start(bf16[512,896]{1,0:T(8,128)(2,1)S(1)} %shard_map.165), channel_id=1, source_target_pairs={{0,16},{8,24},{16,0},{24,8},{1,17},{9,25},{17,1},{25,9},{2,18},{10... | collective-permute-start | bytes 2752520 | tf_op jit(solution)/shard_map/ppermute | solution.py:276
  27.5 21.2 %copy-start.9 = (f32[1,896,512]{2,1,0:T(8,128)S(1)}, f32[1,896,512]{2,1,0:T(8,128)}, u32[]{:S(2)}) copy-start(f32[1,896,512]{2,1,0:T(8,128)} %param.12) | copy-start | bytes 5505028
  27.5 36.3 %collective-permute-start.6 = (bf16[672,512]{1,0:T(8,128)(2,1)S(1)}, bf16[672,512]{1,0:T(8,128)(2,1)S(1)}, u32[]{:S(2)}, u32[]{:S(2)}) collective-permute-start(bf16[672,512]{1,0:T(8,128)(2,1)S(1)} %get-tuple-element.22), channel_id=1, source_target_pairs={{0,16},{8,24},{16,0},{24,8},{1,17},{9,25},{17,1},{25,9},{2,18},{10... | collective-permute-start | bytes 2064392 | tf_op jit(solution)/shard_map/ppermute | solution.py:276
  30.2 33.9 %collective-permute-start.7 = (bf16[384,896]{1,0:T(8,128)(2,1)S(1)}, bf16[384,896]{1,0:T(8,128)(2,1)S(1)}, u32[]{:S(2)}, u32[]{:S(2)}) collective-permute-start(bf16[384,896]{1,0:T(8,128)(2,1)S(1)} %get-tuple-element.23), channel_id=1, source_target_pairs={{0,8},{8,0},{16,24},{24,16},{1,9},{9,1},{17,25},{25,17},{2,10},{10... | collective-permute-start | bytes 2064392 | tf_op jit(solution)/shard_map/ppermute | solution.py:276
  31.9 35.8 %collective-permute-start.2 = (bf16[224,512]{1,0:T(8,128)(2,1)S(1)}, bf16[224,512]{1,0:T(8,128)(2,1)S(1)}, u32[]{:S(2)}, u32[]{:S(2)}) collective-permute-start(bf16[224,512]{1,0:T(8,128)(2,1)S(1)} %get-tuple-element.20), channel_id=1, source_target_pairs={{0,16},{8,24},{16,0},{24,8},{1,17},{9,25},{17,1},{25,9},{2,18},{10... | collective-permute-start | bytes 688136 | tf_op jit(solution)/shard_map/ppermute | solution.py:276
  46.7 21.0 %collective-permute-start.5 = (bf16[128,896]{1,0:T(8,128)(2,1)S(1)}, bf16[128,896]{1,0:T(8,128)(2,1)S(1)}, u32[]{:S(2)}, u32[]{:S(2)}) collective-permute-start(bf16[128,896]{1,0:T(8,128)(2,1)S(1)} %get-tuple-element.21), channel_id=1, source_target_pairs={{0,8},{8,0},{16,24},{24,16},{1,9},{9,1},{17,25},{25,17},{2,10},{10... | collective-permute-start | bytes 688136 | tf_op jit(solution)/shard_map/ppermute | solution.py:276
  48.7 1.5 copy-start.10
  64.1 16.8 %copy-start.8 = (f32[1,512,896]{2,1,0:T(8,128)S(1)}, f32[1,512,896]{2,1,0:T(8,128)}, u32[]{:S(2)}) copy-start(f32[1,512,896]{2,1,0:T(8,128)} %param.19) | copy-start | bytes 5505028
  64.5 16.5 %copy-start.6 = (f32[1,512,896]{2,1,0:T(8,128)S(1)}, f32[1,512,896]{2,1,0:T(8,128)}, u32[]{:S(2)}) copy-start(f32[1,512,896]{2,1,0:T(8,128)} %param.15) | copy-start | bytes 5505028
  64.5 16.5 %copy-start.7 = (f32[1,512,896]{2,1,0:T(8,128)S(1)}, f32[1,512,896]{2,1,0:T(8,128)}, u32[]{:S(2)}) copy-start(f32[1,512,896]{2,1,0:T(8,128)} %param.17) | copy-start | bytes 5505028
  81.0 3.1 %copy-start.3 = (f32[1,896,512]{2,1,0:T(8,128)S(1)}, f32[1,896,512]{2,1,0:T(8,128)}, u32[]{:S(2)}) copy-start(f32[1,896,512]{2,1,0:T(8,128)} %param.14) | copy-start | bytes 5505028
  81.0 3.1 %copy-start.4 = (f32[1,896,512]{2,1,0:T(8,128)S(1)}, f32[1,896,512]{2,1,0:T(8,128)}, u32[]{:S(2)}) copy-start(f32[1,896,512]{2,1,0:T(8,128)} %param.16) | copy-start | bytes 5505028
  81.0 3.1 %copy-start.5 = (f32[1,896,512]{2,1,0:T(8,128)S(1)}, f32[1,896,512]{2,1,0:T(8,128)}, u32[]{:S(2)}) copy-start(f32[1,896,512]{2,1,0:T(8,128)} %param.18) | copy-start | bytes 5505028
  83.4 22.7 %collective-permute-start.14 = (bf16[384,896]{1,0:T(8,128)(2,1)S(1)}, bf16[384,896]{1,0:T(8,128)(2,1)S(1)}, u32[]{:S(2)}, u32[]{:S(2)}) collective-permute-start(bf16[384,896]{1,0:T(8,128)(2,1)S(1)} %shard_map.179.refs_1_), channel_id=1, source_target_pairs={{0,16},{8,24},{16,0},{24,8},{1,17},{9,25},{17,1},{25,9},{2,18},{10... | collective-permute-start | bytes 2064392 | tf_op jit(solution)/shard_map/ppermute | solution.py:276
  86.4 20.3 %collective-permute-start.9 = (bf16[672,512]{1,0:T(8,128)(2,1)S(1)}, bf16[672,512]{1,0:T(8,128)(2,1)S(1)}, u32[]{:S(2)}, u32[]{:S(2)}) collective-permute-start(bf16[672,512]{1,0:T(8,128)(2,1)S(1)} %shard_map.173.refs_1_), channel_id=1, source_target_pairs={{0,8},{8,0},{16,24},{24,16},{1,9},{9,1},{17,25},{25,17},{2,10},{10... | collective-permute-start | bytes 2064392 | tf_op jit(solution)/shard_map/ppermute | solution.py:276
  87.9 17.7 %collective-permute-start.13 = (bf16[128,896]{1,0:T(8,128)(2,1)S(1)}, bf16[128,896]{1,0:T(8,128)(2,1)S(1)}, u32[]{:S(2)}, u32[]{:S(2)}) collective-permute-start(bf16[128,896]{1,0:T(8,128)(2,1)S(1)} %shard_map.178.refs_0_), channel_id=1, source_target_pairs={{0,16},{8,24},{16,0},{24,8},{1,17},{9,25},{17,1},{25,9},{2,18},{10... | collective-permute-start | bytes 688136 | tf_op jit(solution)/shard_map/ppermute | solution.py:276
  89.4 20.4 %collective-permute-start.15 = (bf16[128,896]{1,0:T(8,128)(2,1)S(1)}, bf16[128,896]{1,0:T(8,128)(2,1)S(1)}, u32[]{:S(2)}, u32[]{:S(2)}) collective-permute-start(bf16[128,896]{1,0:T(8,128)(2,1)S(1)} %shard_map.178.refs_0_), channel_id=1, source_target_pairs={{0,8},{8,0},{16,24},{24,16},{1,9},{9,1},{17,25},{25,17},{2,10},{10... | collective-permute-start | bytes 688136 | tf_op jit(solution)/shard_map/ppermute | solution.py:276
  90.8 58.7 %collective-permute-start.16 = (bf16[384,896]{1,0:T(8,128)(2,1)S(1)}, bf16[384,896]{1,0:T(8,128)(2,1)S(1)}, u32[]{:S(2)}, u32[]{:S(2)}) collective-permute-start(bf16[384,896]{1,0:T(8,128)(2,1)S(1)} %shard_map.179.refs_1_), channel_id=1, source_target_pairs={{0,8},{8,0},{16,24},{24,16},{1,9},{9,1},{17,25},{25,17},{2,10},{10... | collective-permute-start | bytes 2064392 | tf_op jit(solution)/shard_map/ppermute | solution.py:276
  105.6 60.9 %collective-permute-start.11 = (bf16[672,512]{1,0:T(8,128)(2,1)S(1)}, bf16[672,512]{1,0:T(8,128)(2,1)S(1)}, u32[]{:S(2)}, u32[]{:S(2)}) collective-permute-start(bf16[672,512]{1,0:T(8,128)(2,1)S(1)} %shard_map.173.refs_1_), channel_id=1, source_target_pairs={{0,16},{8,24},{16,0},{24,8},{1,17},{9,25},{17,1},{25,9},{2,18},{10... | collective-permute-start | bytes 2064392 | tf_op jit(solution)/shard_map/ppermute | solution.py:276
  106.1 61.9 %collective-permute-start.17 = (bf16[384,896]{1,0:T(8,128)(2,1)S(1)}, bf16[384,896]{1,0:T(8,128)(2,1)S(1)}, u32[]{:S(2)}, u32[]{:S(2)}) collective-permute-start(bf16[384,896]{1,0:T(8,128)(2,1)S(1)} %collective-permute-done.14.refs_2_), channel_id=1, source_target_pairs={{0,8},{8,0},{16,24},{24,16},{1,9},{9,1},{17,25},{25,17},{2,10},{10... | collective-permute-start | bytes 2064392 | tf_op jit(solution)/shard_map/ppermute | solution.py:276
  106.7 62.7 %collective-permute-start.12 = (bf16[672,512]{1,0:T(8,128)(2,1)S(1)}, bf16[672,512]{1,0:T(8,128)(2,1)S(1)}, u32[]{:S(2)}, u32[]{:S(2)}) collective-permute-start(bf16[672,512]{1,0:T(8,128)(2,1)S(1)} %collective-permute-done.9.refs_2_), channel_id=1, source_target_pairs={{0,16},{8,24},{16,0},{24,8},{1,17},{9,25},{17,1},{25,9},{2,18},{10... | collective-permute-start | bytes 2064392 | tf_op jit(solution)/shard_map/ppermute | solution.py:276
  109.7 33.0 %collective-permute-start.8 = (bf16[224,512]{1,0:T(8,128)(2,1)S(1)}, bf16[224,512]{1,0:T(8,128)(2,1)S(1)}, u32[]{:S(2)}, u32[]{:S(2)}) collective-permute-start(bf16[224,512]{1,0:T(8,128)(2,1)S(1)} %shard_map.172.refs_0_), channel_id=1, source_target_pairs={{0,8},{8,0},{16,24},{24,16},{1,9},{9,1},{17,25},{25,17},{2,10},{10... | collective-permute-start | bytes 688136 | tf_op jit(solution)/shard_map/ppermute | solution.py:276
  142.7 6.2 %collective-permute-start.10 = (bf16[224,512]{1,0:T(8,128)(2,1)S(1)}, bf16[224,512]{1,0:T(8,128)(2,1)S(1)}, u32[]{:S(2)}, u32[]{:S(2)}) collective-permute-start(bf16[224,512]{1,0:T(8,128)(2,1)S(1)} %shard_map.172.refs_0_), channel_id=1, source_target_pairs={{0,16},{8,24},{16,0},{24,8},{1,17},{9,25},{17,1},{25,9},{2,18},{10... | collective-permute-start | bytes 688136 | tf_op jit(solution)/shard_map/ppermute | solution.py:276
  148.9 22.0 %collective-permute-start.19 = (bf16[128,896]{1,0:T(8,128)(2,1)S(1)}, bf16[128,896]{1,0:T(8,128)(2,1)S(1)}, u32[]{:S(2)}, u32[]{:S(2)}) collective-permute-start(bf16[128,896]{1,0:T(8,128)(2,1)S(1)} %collective-permute-done.13.refs_1_), channel_id=1, source_target_pairs={{0,8},{8,0},{16,24},{24,16},{1,9},{9,1},{17,25},{25,17},{2,10},{10... | collective-permute-start | bytes 688136 | tf_op jit(solution)/shard_map/ppermute | solution.py:276
  149.5 21.4 %collective-permute-start.18 = (bf16[224,512]{1,0:T(8,128)(2,1)S(1)}, bf16[224,512]{1,0:T(8,128)(2,1)S(1)}, u32[]{:S(2)}, u32[]{:S(2)}) collective-permute-start(bf16[224,512]{1,0:T(8,128)(2,1)S(1)} %collective-permute-done.8.refs_1_), channel_id=1, source_target_pairs={{0,16},{8,24},{16,0},{24,8},{1,17},{9,25},{17,1},{25,9},{2,18},{10... | collective-permute-start | bytes 688136 | tf_op jit(solution)/shard_map/ppermute | solution.py:276
where the time goes:
time: 172 us
  waiting for transfers between devices  96.9 us (56%)
  Pallas kernels  30.6 us (18%)
  starting transfers between devices  27 us (16%)
  blocking collectives  13.1 us (8%)
  local copies, waits for them, and re-layouts  3.23 us (2%)
    ppermute x20, waiting for transfers between devices, exchange(): return lax.ppermute(value, 'dp', [(i, i ^ partner) for i in range(parts)])  96.9 us
    ppermute x20, starting transfers between devices, exchange(): return lax.ppermute(value, 'dp', [(i, i ^ partner) for i in range(parts)])  27 us
    all_to_all x1, blocking collectives, on_square(): sums = lax.all_to_all(sums, ('dp', 'mp'), 0, 0, tiled=True)  13.1 us
    pallas_call x6, Pallas kernels, place(): call(place_body, BLOCKS, ([] if first else [pl.BlockSpec(memory_space=pl....  9.02 us
    pallas_call x2, Pallas kernels, update(): call(functools.partial(update_body, entries), BLOCKS, [pl.BlockSpec(sums....  8.24 us
    pallas_call x4, Pallas kernels, weight_piece(): call(functools.partial(weight_body, entries), blocks, [pl.BlockSpec(sums....  6.28 us
  transfers between devices with their start and end apart: 20, of which 8 were waited for; matrix products, arithmetic and copies ran while one was open for 0% of the time, Pallas kernels for 16%

commit v1 on v0

--- a/solution.py
+++ b/solution.py
@@ -18,6 +18,8 @@
 
 BLOCKS = 4
 HEAD = 1
+
+CUT_GRANT = 8
 
 
 def adamw(total, clip, master, moment, second):
@@ -30,6 +32,17 @@
     return (master - learn_rate * (update + weight_decay * master), first, variance)
 
 
+KEEP = 1.0 - learn_rate * weight_decay
+FIRST = learn_rate / (1.0 - beta_one**STEP)
+SECOND = 1.0 / (1.0 - beta_two**STEP)
+
+
+def shard_of(kept, pull, spread, scaled):
+    step = pull + (FIRST * (1.0 - beta_one)) * scaled
+    width = jnp.sqrt(spread + (SECOND * (1.0 - beta_two)) * (scaled * scaled)) + adam_eps
+    return kept - step / width
+
+
 class Layout:
     def __init__(self, rows, cols, axis, parts):
         self.rows, self.cols, self.axis, self.parts = rows, cols, axis, parts
@@ -44,6 +57,11 @@
 
         return pl.BlockSpec(self.block, index)
 
+    def quarter(self, ref, owner):
+        if self.axis == 0:
+            return ref.at[pl.ds(pl.multiple_of(owner * self.rows, self.rows), self.rows), :]
+        return ref.at[:, pl.ds(pl.multiple_of(owner * self.cols, self.cols), self.cols)]
+
     def shard(self, start=0):
         return pl.BlockSpec(self.block, lambda i: (start + i, 0))
 
@@ -60,7 +78,7 @@
         return blocks * self.step * self.cols * width
 
 
-def call(body, grid, in_specs, out_specs, out_shape, cost, aliases=None):
+def call(body, grid, in_specs, out_specs, out_shape, cost, aliases=None, grant=24):
     return pl.pallas_call(
         body,
         grid=(grid,),
@@ -69,20 +87,38 @@
         out_shape=out_shape,
         input_output_aliases=aliases or {},
         compiler_params=pltpu.CompilerParams(
-            dimension_semantics=("arbitrary",), vmem_limit_bytes=24 * 2**20
+            dimension_semantics=("arbitrary",), vmem_limit_bytes=grant * 2**20
         ),
         cost_estimate=pl.CostEstimate(flops=cost * 2, bytes_accessed=cost, transcendentals=0),
     )
 
 
-def copy_body(source, target):
-    target[...] = source[...]
-
-
-def extract(lay, grads, partner):
-    return call(
-        copy_body, BLOCKS, [lay.piece(partner)], lay.shard(), lay.array(BLOCKS, jnp.bfloat16), lay.bytes(BLOCKS, 4)
-    )(grads)
+def cut_body(lays, partners, grads_one, grads_two, out_one, out_two, sems):
+    me = lax.axis_index("dp")
+    copies = [
+        pltpu.make_async_copy(lay.quarter(grads, me ^ partner), out, sems.at[k])
+        for k, (lay, partner, grads, out) in enumerate(
+            zip(lays, partners, (grads_one, grads_two), (out_one, out_two))
+        )
+    ]
+    for copy in copies:
+        copy.start()
+    for copy in copies:
+        copy.wait()
+
+
+def cut(lays, grads, partners):
+    size = sum(lay.bytes(BLOCKS, 2) for lay in lays)
+    return pl.pallas_call(
+        functools.partial(cut_body, lays, partners),
+        in_specs=[pl.BlockSpec(memory_space=pltpu.HBM)] * 2,
+        out_specs=[pl.BlockSpec(memory_space=pltpu.VMEM)] * 2,
+        out_shape=[pltpu.VMEM((lay.rows, lay.cols), jnp.bfloat16) for lay in lays],
+        scratch_shapes=[pltpu.SemaphoreType.DMA((2,))],
+        compiler_params=pltpu.CompilerParams(vmem_limit_bytes=CUT_GRANT * 2**20),
+        cost_estimate=pl.CostEstimate(flops=size, bytes_accessed=2 * size, transcendentals=0),
+        name="cut",
+    )(*(pltpu.with_memory_space_constraint(g, pltpu.HBM) for g in grads))
 
 
 def add_body(grads, arrived, short, long):
@@ -124,19 +160,37 @@
     )(grads, arrived, accum)
 
 
-def squares(held, arrived):
+def ready_body(master, moment, second, kept, pull, spread):
+    kept[...] = KEEP * master[...]
+    pull[...] = (FIRST * beta_one) * moment[...]
+    spread[...] = (SECOND * beta_two) * second[...]
+
+
+def ready(lay, state):
+    return call(
+        ready_body,
+        BLOCKS,
+        [lay.shard()] * 3,
+        [lay.shard()] * 3,
+        [lay.array(BLOCKS, jnp.float32)] * 3,
+        lay.bytes(BLOCKS, 24),
+    )(*state)
+
+
+def squares(held, arrived, out):
     total = held[...] + arrived[...].astype(jnp.float32)
+    out[...] = total
     rows, cols = total.shape
     tile = jnp.sum((total * total).reshape(rows // 8, 8, cols), axis=0)
     return sum(tile[:, k : k + 128] for k in range(0, cols, 128))
 
 
-def long_body(held, arrived, out):
+def long_body(held, arrived, total, out):
     @pl.when(pl.program_id(0) == 0)
     def _():
         out[...] = jnp.zeros_like(out)
 
-    out[...] += squares(held, arrived)
+    out[...] += squares(held, arrived, total)
 
 
 def long_squares(lay, held, arrived):
@@ -145,14 +199,14 @@
         long_body,
         n,
         [lay.shard(HEAD), lay.shard()],
-        pl.BlockSpec((8, 128), lambda i: (0, 0)),
-        jax.ShapeDtypeStruct((8, 128), jnp.float32),
-        lay.bytes(n, 6),
+        [lay.shard(), pl.BlockSpec((8, 128), lambda i: (0, 0))],
+        [lay.array(n, jnp.float32), jax.ShapeDtypeStruct((8, 128), jnp.float32)],
+        lay.bytes(n, 10),
     )(held, arrived)
 
 
-def short_body(held_one, arrived_one, held_two, arrived_two, sum_one, sum_two, out):
-    value = squares(held_one, arrived_one) + squares(held_two, arrived_two)
+def short_body(held_one, arrived_one, held_two, arrived_two, sum_one, sum_two, total_one, total_two, out):
+    value = squares(held_one, arrived_one, total_one) + squares(held_two, arrived_two, total_two)
 
     @pl.when(pl.program_id(0) == 0)
     def _():
@@ -164,14 +218,15 @@
 def short_squares(lays, helds, arriveds, sums, devices):
     tile = pl.BlockSpec((8, 128), lambda i: (0, 0))
     one, two = lays
-    return call(
+    *totals, sums = call(
         short_body,
         HEAD,
         [one.shard(), one.shard(), two.shard(), two.shard(), tile, tile],
-        pl.BlockSpec((devices, 128), lambda i: (0, 0)),
-        jax.ShapeDtypeStruct((devices, 128), jnp.float32),
-        one.bytes(HEAD, 12),
+        [one.shard(), two.shard(), pl.BlockSpec((devices, 128), lambda i: (0, 0))],
+        [lay.array(HEAD, jnp.float32) for lay in lays] + [jax.ShapeDtypeStruct((devices, 128), jnp.float32)],
+        one.bytes(HEAD, 20),
     )(helds[0], arriveds[0], helds[1], arriveds[1], *sums)
+    return totals, sums
 
 
 def clip_of(entries, sums):
@@ -179,44 +234,40 @@
     return jnp.minimum(1.0, lax.rsqrt(sumsq / entries + 1e-06))
 
 
-def weight_body(entries, sums, held, arrived, master, moment, second, out):
-    total = held[...] + arrived[...].astype(jnp.float32)
-    shard, _, _ = adamw(total, clip_of(entries, sums), master[...], moment[...], second[...])
-    out[...] = shard.astype(jnp.bfloat16)
-
-
-def weight_piece(lay, start, blocks, entries, sums, held, arrived, state):
+def weight_body(entries, sums, total, kept, pull, spread, out):
+    scaled = clip_of(entries, sums) * total[...]
+    out[...] = shard_of(kept[...], pull[...], spread[...], scaled).astype(jnp.bfloat16)
+
+
+def weight_piece(lay, start, blocks, entries, sums, total, terms):
     return call(
         functools.partial(weight_body, entries),
         blocks,
-        [pl.BlockSpec(sums.shape, lambda i: (0, 0)), lay.shard(start), lay.shard()] + [lay.shard(start)] * 3,
+        [pl.BlockSpec(sums.shape, lambda i: (0, 0)), lay.shard()] + [lay.shard(start)] * 3,
         lay.shard(),
         lay.array(blocks, jnp.bfloat16),
-        lay.bytes(blocks, 20),
-    )(sums, held, arrived, *state)
-
-
-def update_body(entries, sums, held, short, long, master, moment, second, shard_out, first_out, variance_out):
-    arrived = jnp.where(
-        pl.program_id(0) < HEAD, short[...].astype(jnp.float32), long[...].astype(jnp.float32)
+        lay.bytes(blocks, 18),
+    )(sums, total, *terms)
+
+
+def update_body(entries, sums, short, long, master, moment, second, shard_out, first_out, variance_out):
+    scaled = clip_of(entries, sums) * jnp.where(pl.program_id(0) < HEAD, short[...], long[...])
+    shard_out[...] = shard_of(
+        KEEP * master[...], (FIRST * beta_one) * moment[...], (SECOND * beta_two) * second[...], scaled
     )
-    shard, first, variance = adamw(
-        held[...] + arrived, clip_of(entries, sums), master[...], moment[...], second[...]
-    )
-    shard_out[...] = shard
-    first_out[...] = first
-    variance_out[...] = variance
-
-
-def update(lay, entries, sums, held, short, long, state):
+    first_out[...] = beta_one * moment[...] + (1.0 - beta_one) * scaled
+    variance_out[...] = beta_two * second[...] + (1.0 - beta_two) * (scaled * scaled)
+
+
+def update(lay, entries, sums, short, long, state):
     return call(
         functools.partial(update_body, entries),
         BLOCKS,
-        [pl.BlockSpec(sums.shape, lambda i: (0, 0)), lay.shard(), lay.short(), lay.long()] + [lay.shard()] * 3,
+        [pl.BlockSpec(sums.shape, lambda i: (0, 0)), lay.short(), lay.long()] + [lay.shard()] * 3,
         [lay.shard()] * 3,
         [lay.array(BLOCKS, jnp.float32)] * 3,
-        lay.bytes(BLOCKS, 30),
-    )(sums, held, short, long, *state)
+        lay.bytes(BLOCKS, 28),
+    )(sums, short, long, *state)
 
 
 def place_body(*refs):
@@ -290,26 +341,27 @@
     def move(values, partners):
         return [exchange(values[k], partners[k], parts) for k in both]
 
-    relayed = move(step(extract, grads, (3, 3)), near)
-    direct = move(step(extract, grads, near), near)
+    relayed = move(cut(lays, grads, (3, 3)), near)
+    direct = move(cut(lays, grads, near), near)
     sent = step(add_forward, grads, relayed, far)
     tail = move([x[1] for x in sent], far)
     head = move([x[0] for x in sent], far)
     held = step(partial_sum, grads, direct, accums)
-    sums = step(long_squares, held, tail)
-    sums = short_squares(lays, held, head, sums, devices)
+    terms = step(ready, states)
+    tail_totals, sums = zip(*step(long_squares, held, tail))
+    head_totals, sums = short_squares(lays, held, head, sums, devices)
     sums = lax.all_to_all(sums, ("dp", "mp"), 0, 0, tiled=True)
 
     def weights(start, blocks):
-        return lambda lay, held, arrived, state: weight_piece(lay, start, blocks, entries, sums, held, arrived, state)
-
-    own_head = step(weights(0, HEAD), held, head, states)
-    own_tail = step(weights(HEAD, BLOCKS - HEAD), held, tail, states)
+        return lambda lay, total, terms: weight_piece(lay, start, blocks, entries, sums, total, terms)
+
+    own_head = step(weights(0, HEAD), head_totals, terms)
+    own_tail = step(weights(HEAD, BLOCKS - HEAD), tail_totals, terms)
     near_head, near_tail = move(own_head, near), move(own_tail, near)
     far_tail, far_head = move(own_tail, far), move(own_head, far)
     last_tail, last_head = move(near_tail, far), move(near_head, far)
 
-    updated = step(lambda lay, *x: update(lay, entries, sums, *x), held, head, tail, states)
+    updated = step(lambda lay, *x: update(lay, entries, sums, *x), head_totals, tail_totals, states)
     wholes = step(place, (None, None), own_head, own_tail, (0, 0))
     wholes = step(place, wholes, near_head, near_tail, near)
     wholes = step(place, wholes, far_head, far_tail, far)

time: 172 us -> 186 us (1.081)
  local copies, waits for them, and re-layouts: 3.23 us -> 23.4 us
  blocking collectives: 13.1 us -> 0 us
  starting transfers between devices: 27 us -> 32.6 us
    unnamed x22 -> x74, local copies, waits for them, and re-layouts: 3.23 us -> 23.4 us
    all_to_all x1 -> x0, blocking collectives: 13.1 us -> none  [on_square(): sums = lax.all_to_all(sums, ('dp', 'mp'), 0, 0, tiled=True)]
    all_to_all x0 -> x1, starting transfers between devices: none -> 4.92 us  [on_square(): sums = lax.all_to_all(sums, ('dp', 'mp'), 0, 0, tiled=True)]
    pallas_call x6, Pallas kernels: 1.44 us -> 4.68 us  [the longest x2 3.11 us: cut(): pl.pallas_call(functools.partial(cut_body, lays, partners), in_specs=[pl....]
    pallas_call x4, Pallas kernels: 6.28 us -> 3.38 us  [weight_piece(): call(functools.partial(weight_body, entries), blocks, [pl.BlockSpec(sums....]
  transfers between devices with their start and end apart: 20 -> 21, of which waited for: 8 -> 7; matrix products, arithmetic and copies ran while one was open for 0% -> 0% of each run, Pallas kernels for 16% -> 14%
where the time goes in v1:
time: 186 us
  waiting for transfers between devices  97.4 us (52%)
  starting transfers between devices  32.6 us (18%)
  Pallas kernels  31.2 us (17%)
  local copies, waits for them, and re-layouts  23.4 us (13%)
    ppermute x20, waiting for transfers between devices, exchange(): return lax.ppermute(value, 'dp', [(i, i ^ partner) for i in range(parts)])  97.4 us
    ppermute x20, starting transfers between devices, exchange(): return lax.ppermute(value, 'dp', [(i, i ^ partner) for i in range(parts)])  27.7 us
    unnamed x74, local copies, waits for them, and re-layouts  23.4 us
    pallas_call x6, Pallas kernels, place(): call(place_body, BLOCKS, ([] if first else [pl.BlockSpec(memory_space=pl....  9.02 us
    pallas_call x2, Pallas kernels, update(): call(functools.partial(update_body, entries), BLOCKS, [pl.BlockSpec(sums....  7.9 us
    all_to_all x1, starting transfers between devices, on_square(): sums = lax.all_to_all(sums, ('dp', 'mp'), 0, 0, tiled=True)  4.92 us
  transfers between devices with their start and end apart: 21, of which 7 were waited for; matrix products, arithmetic and copies ran while one was open for 0% of the time, Pallas kernels for 14%

profile of v1, /device:TPU:0, one launch (start us, length us, event | category | flops | bytes accessed | tf_op | source)
XLA Modules:
  0.0 185.6 jit_solution(6651830080684994269)
XLA Ops:
  0.6 1.5 cut.3
  2.1 3.0 %collective-permute-start.1 = (bf16[896,512]{1,0:T(8,128)(2,1)S(1)}, bf16[896,512]{1,0:T(8,128)(2,1)S(1)}, u32[]{:S(2)}, u32[]{:S(2)}) collective-permute-start(bf16[896,512]{1,0:T(8,128)(2,1)S(1)} %get-tuple-element.38), channel_id=1, source_target_pairs={{0,8},{8,0},{16,24},{24,16},{1,9},{9,1},{17,25},{25,17},{2,10},{10... | collective-permute-start | bytes 2752520 | tf_op jit(solution)/shard_map/ppermute | solution.py:327
  5.2 1.5 collective-permute-start.4
  6.7 1.6 cut.2
  8.3 0.6 collective-permute-start
  9.0 17.4 %collective-permute-done.1.arrived = bf16[896,512]{1,0:T(8,128)(2,1)S(1)} collective-permute-done((bf16[896,512]{1,0:T(8,128)(2,1)S(1)}, bf16[896,512]{1,0:T(8,128)(2,1)S(1)}, u32[]{:S(2)}, u32[]{:S(2)}) %collective-permute-start.1) | collective-permute-done | bytes 917536 | tf_op jit(solution)/shard_map/ppermute | solution.py:327
  26.8 2.1 %collective-permute-start.6 = (bf16[672,512]{1,0:T(8,128)(2,1)S(1)}, bf16[672,512]{1,0:T(8,128)(2,1)S(1)}, u32[]{:S(2)}, u32[]{:S(2)}) collective-permute-start(bf16[672,512]{1,0:T(8,128)(2,1)S(1)} %get-tuple-element.43), channel_id=1, source_target_pairs={{0,16},{8,24},{16,0},{24,8},{1,17},{9,25},{17,1},{25,9},{2,18},{10... | collective-permute-start | bytes 2064392 | tf_op jit(solution)/shard_map/ppermute | solution.py:327
  29.0 0.6 shard_map.164
  29.5 1.6 collective-permute-start.7
  31.6 14.4 %collective-permute-done.arrived = bf16[896,512]{1,0:T(8,128)(2,1)S(1)} collective-permute-done((bf16[896,512]{1,0:T(8,128)(2,1)S(1)}, bf16[896,512]{1,0:T(8,128)(2,1)S(1)}, u32[]{:S(2)}, u32[]{:S(2)}) %collective-permute-start) | collective-permute-done | bytes 917536 | tf_op jit(solution)/shard_map/ppermute | solution.py:327
  46.0 2.0 %collective-permute-start.5 = (bf16[128,896]{1,0:T(8,128)(2,1)S(1)}, bf16[128,896]{1,0:T(8,128)(2,1)S(1)}, u32[]{:S(2)}, u32[]{:S(2)}) collective-permute-start(bf16[128,896]{1,0:T(8,128)(2,1)S(1)} %get-tuple-element.42), channel_id=1, source_target_pairs={{0,8},{8,0},{16,24},{24,16},{1,9},{9,1},{17,25},{25,17},{2,10},{10... | collective-permute-start | bytes 688136 | tf_op jit(solution)/shard_map/ppermute | solution.py:327
  48.4 1.2 copy-done.36
  50.0 12.8 %collective-permute-done.6.arrived = bf16[672,512]{1,0:T(8,128)(2,1)S(1)} collective-permute-done((bf16[672,512]{1,0:T(8,128)(2,1)S(1)}, bf16[672,512]{1,0:T(8,128)(2,1)S(1)}, u32[]{:S(2)}, u32[]{:S(2)}) %collective-permute-start.6) | collective-permute-done | bytes 688160 | tf_op jit(solution)/shard_map/ppermute | solution.py:327
  63.3 1.1 copy-done.28
  64.4 1.9 %collective-permute-done.2.arrived_one = bf16[224,512]{1,0:T(8,128)(2,1)S(1)} collective-permute-done((bf16[224,512]{1,0:T(8,128)(2,1)S(1)}, bf16[224,512]{1,0:T(8,128)(2,1)S(1)}, u32[]{:S(2)}, u32[]{:S(2)}) %collective-permute-start.2) | collective-permute-done | bytes 229408 | tf_op jit(solution)/shard_map/ppermute | solution.py:327
  66.3 0.8 shard_map.167
  67.1 0.8 copy-done.31
  67.9 0.8 copy-done.33
  68.6 4.9 %all-to-all-start = ((f32[32,1,128]{2,1,0:T(1,128)}), f32[32,1,128]{2,1,0:T(1,128)S(1)}, u32[]{:S(2)}, u32[]{:S(2)}) async-start(f32[32,1,128]{2,1,0:T(1,128)} %bitcast.5), calls=%async_computation | async-start | bytes 32768 | tf_op jit(solution)/shard_map/all_to_all | solution.py:353
  73.6 1.5 copy-done.7
  75.1 1.5 copy-done.9
  76.6 1.5 copy-done.11
  78.1 0.5 shard_map.175
  78.6 1.2 copy-done.19
  79.8 1.2 copy-done.22
  81.1 1.2 copy-done.25
  82.3 0.5 shard_map.168
  82.9 1.2 copy-done.13
  84.1 1.2 copy-done.15
  85.3 1.2 copy-done.17
  86.6 1.5 copy-done.20
  88.1 1.5 copy-done.23
  89.6 1.5 copy-done.26
  91.1 1.3 copy-done.29
  92.4 1.3 shard_map.177.refs_1_
  93.7 1.8 collective-permute-start.14
  95.6 1.3 shard_map.170.refs_1_
  96.8 1.5 collective-permute-start.9
  98.8 1.3 collective-permute-start.13
  100.1 1.3 collective-permute-start.15
  101.4 0.7 collective-permute-start.16
  102.1 14.1 %collective-permute-done.13.refs_1_ = bf16[128,896]{1,0:T(8,128)(2,1)S(1)} collective-permute-done((bf16[128,896]{1,0:T(8,128)(2,1)S(1)}, bf16[128,896]{1,0:T(8,128)(2,1)S(1)}, u32[]{:S(2)}, u32[]{:S(2)}) %collective-permute-start.13) | collective-permute-done | bytes 229408 | tf_op jit(solution)/shard_map/ppermute | solution.py:327
  116.2 1.6 collective-permute-start.11
  117.9 1.5 collective-permute-start.17
  119.3 0.6 collective-permute-start.12
  120.3 1.2 collective-permute-start.8
  121.6 31.8 %collective-permute-done.8.refs_1_ = bf16[224,512]{1,0:T(8,128)(2,1)S(1)} collective-permute-done((bf16[224,512]{1,0:T(8,128)(2,1)S(1)}, bf16[224,512]{1,0:T(8,128)(2,1)S(1)}, u32[]{:S(2)}, u32[]{:S(2)}) %collective-permute-start.8) | collective-permute-done | bytes 229408 | tf_op jit(solution)/shard_map/ppermute | solution.py:327
  153.4 1.5 collective-permute-start.10
  154.9 5.0 %collective-permute-done.10.refs_1_ = bf16[224,512]{1,0:T(8,128)(2,1)S(1)} collective-permute-done((bf16[224,512]{1,0:T(8,128)(2,1)S(1)}, bf16[224,512]{1,0:T(8,128)(2,1)S(1)}, u32[]{:S(2)}, u32[]{:S(2)}) %collective-permute-start.10) | collective-permute-done | bytes 229408 | tf_op jit(solution)/shard_map/ppermute | solution.py:327
  159.9 1.5 collective-permute-start.19
  161.4 1.7 collective-permute-start.18
  163.1 1.5 shard_map.178.refs_0_
  164.7 1.5 shard_map.171.refs_0_
  166.3 0.7 copy-done.6
  167.0 4.0 %shard_map.183 = (f32[896,512]{1,0:T(8,128)}, f32[896,512]{1,0:T(8,128)}, f32[896,512]{1,0:T(8,128)}) custom-call(f32[32,128]{1,0:T(8,128)S(1)} %bitcast.48, f32[224,512]{1,0:T(8,128)S(1)} %copy-done.34, f32[672,512]{1,0:T(8,128)S(1)} %get-tuple-element.52.total.long, f32[896,512]{1,0:T(8,128)S(1)} %bitcast.31, f32[896,512]{1,0:T(8,128)S(1)} %bitcast.33, ...), custom_call_target="tpu_custom_call" | custom-call | flops 25690112 | bytes 12845056 | tf_op jit(solution)/shard_map/pallas_call | solution.py:263
  171.0 0.6 copy-done.12
  172.0 3.9 %shard_map.184 = (f32[512,896]{1,0:T(8,128)}, f32[512,896]{1,0:T(8,128)}, f32[512,896]{1,0:T(8,128)}) custom-call(f32[32,128]{1,0:T(8,128)S(1)} %bitcast.49, f32[128,896]{1,0:T(8,128)S(1)} %copy-done.32, f32[384,896]{1,0:T(8,128)S(1)} %copy-done.30, f32[512,896]{1,0:T(8,128)S(1)} %bitcast.37, f32[512,896]{1,0:T(8,128)S(1)} %bitcast.39, f32[512,896]{1,0:T(8,128)S(1)} %bitcast.41), custom_call_target="tpu_custom_call" | custom-call | flops 25690112 | bytes 12845056 | tf_op jit(solution)/shard_map/pallas_call | solution.py:263
  175.9 1.5 shard_map.179.refs_0_
  177.4 1.5 shard_map.172.refs_0_
  178.9 1.5 shard_map.180._
  180.4 1.5 shard_map.173._
  181.9 1.4 shard_map.181.__
  183.3 1.4 shard_map.174._
  184.8 0.8 shard_map.182
  (78 shorter events, 3.8 us)
Async XLA Ops:
  2.1 24.2 %collective-permute-start.1 = (bf16[896,512]{1,0:T(8,128)(2,1)S(1)}, bf16[896,512]{1,0:T(8,128)(2,1)S(1)}, u32[]{:S(2)}, u32[]{:S(2)}) collective-permute-start(bf16[896,512]{1,0:T(8,128)(2,1)S(1)} %get-tuple-element.38), channel_id=1, source_target_pairs={{0,8},{8,0},{16,24},{24,16},{1,9},{9,1},{17,25},{25,17},{2,10},{10... | collective-permute-start | bytes 2752520 | tf_op jit(solution)/shard_map/ppermute | solution.py:327
  5.2 23.8 %collective-permute-start.4 = (bf16[512,896]{1,0:T(8,128)(2,1)S(1)}, bf16[512,896]{1,0:T(8,128)(2,1)S(1)}, u32[]{:S(2)}, u32[]{:S(2)}) collective-permute-start(bf16[512,896]{1,0:T(8,128)(2,1)S(1)} %get-tuple-element.41), channel_id=1, source_target_pairs={{0,16},{8,24},{16,0},{24,8},{1,17},{9,25},{17,1},{25,9},{2,18},{10... | collective-permute-start | bytes 2752520 | tf_op jit(solution)/shard_map/ppermute | solution.py:327
  6.7 19.7 %copy-start = (bf16[1,1,3584,512]{3,2,1,0:T(8,128)(2,1)S(1)}, bf16[1,1,3584,512]{3,2,1,0:T(8,128)(2,1)}, u32[]{:S(2)}) copy-start(bf16[1,1,3584,512]{3,2,1,0:T(8,128)(2,1)} %param.10) | copy-start | bytes 11010052
  8.3 37.7 %collective-permute-start = (bf16[896,512]{1,0:T(8,128)(2,1)S(1)}, bf16[896,512]{1,0:T(8,128)(2,1)S(1)}, u32[]{:S(2)}, u32[]{:S(2)}) collective-permute-start(bf16[896,512]{1,0:T(8,128)(2,1)S(1)} %get-tuple-element.37), channel_id=1, source_target_pairs={{0,8},{8,0},{16,24},{24,16},{1,9},{9,1},{17,25},{25,17},{2,10},{10... | collective-permute-start | bytes 2752520 | tf_op jit(solution)/shard_map/ppermute | solution.py:327
  8.9 20.1 %copy-start.1 = (bf16[1,1,512,3584]{3,2,1,0:T(8,128)(2,1)S(1)}, bf16[1,1,512,3584]{3,2,1,0:T(8,128)(2,1)}, u32[]{:S(2)}) copy-start(bf16[1,1,512,3584]{3,2,1,0:T(8,128)(2,1)} %param.11) | copy-start | bytes 11010052
  8.9 39.5 %collective-permute-start.3 = (bf16[512,896]{1,0:T(8,128)(2,1)S(1)}, bf16[512,896]{1,0:T(8,128)(2,1)S(1)}, u32[]{:S(2)}, u32[]{:S(2)}) collective-permute-start(bf16[512,896]{1,0:T(8,128)(2,1)S(1)} %get-tuple-element.40), channel_id=1, source_target_pairs={{0,16},{8,24},{16,0},{24,8},{1,17},{9,25},{17,1},{25,9},{2,18},{10... | collective-permute-start | bytes 2752520 | tf_op jit(solution)/shard_map/ppermute | solution.py:327
  26.8 21.2 %copy-start.35 = (f32[1,896,512]{2,1,0:T(8,128)S(1)}, f32[1,896,512]{2,1,0:T(8,128)}, u32[]{:S(2)}) copy-start(f32[1,896,512]{2,1,0:T(8,128)} %param.12) | copy-start | bytes 5505028
  26.8 35.9 %collective-permute-start.6 = (bf16[672,512]{1,0:T(8,128)(2,1)S(1)}, bf16[672,512]{1,0:T(8,128)(2,1)S(1)}, u32[]{:S(2)}, u32[]{:S(2)}) collective-permute-start(bf16[672,512]{1,0:T(8,128)(2,1)S(1)} %get-tuple-element.43), channel_id=1, source_target_pairs={{0,16},{8,24},{16,0},{24,8},{1,17},{9,25},{17,1},{25,9},{2,18},{10... | collective-permute-start | bytes 2064392 | tf_op jit(solution)/shard_map/ppermute | solution.py:327
  29.5 33.5 %collective-permute-start.7 = (bf16[384,896]{1,0:T(8,128)(2,1)S(1)}, bf16[384,896]{1,0:T(8,128)(2,1)S(1)}, u32[]{:S(2)}, u32[]{:S(2)}) collective-permute-start(bf16[384,896]{1,0:T(8,128)(2,1)S(1)} %get-tuple-element.45), channel_id=1, source_target_pairs={{0,8},{8,0},{16,24},{24,16},{1,9},{9,1},{17,25},{25,17},{2,10},{10... | collective-permute-start | bytes 2064392 | tf_op jit(solution)/shard_map/ppermute | solution.py:327
  31.1 35.2 %collective-permute-start.2 = (bf16[224,512]{1,0:T(8,128)(2,1)S(1)}, bf16[224,512]{1,0:T(8,128)(2,1)S(1)}, u32[]{:S(2)}, u32[]{:S(2)}) collective-permute-start(bf16[224,512]{1,0:T(8,128)(2,1)S(1)} %get-tuple-element.39), channel_id=1, source_target_pairs={{0,16},{8,24},{16,0},{24,8},{1,17},{9,25},{17,1},{25,9},{2,18},{10... | collective-permute-start | bytes 688136 | tf_op jit(solution)/shard_map/ppermute | solution.py:327
  46.0 20.3 %collective-permute-start.5 = (bf16[128,896]{1,0:T(8,128)(2,1)S(1)}, bf16[128,896]{1,0:T(8,128)(2,1)S(1)}, u32[]{:S(2)}, u32[]{:S(2)}) collective-permute-start(bf16[128,896]{1,0:T(8,128)(2,1)S(1)} %get-tuple-element.42), channel_id=1, source_target_pairs={{0,8},{8,0},{16,24},{24,16},{1,9},{9,1},{17,25},{25,17},{2,10},{10... | collective-permute-start | bytes 688136 | tf_op jit(solution)/shard_map/ppermute | solution.py:327
  48.0 1.5 copy-start.36
  63.3 1.1 copy-start.28
  67.1 0.8 copy-start.31
  67.9 0.8 copy-start.33
  68.6 17.9 %all-to-all-start = ((f32[32,1,128]{2,1,0:T(1,128)}), f32[32,1,128]{2,1,0:T(1,128)S(1)}, u32[]{:S(2)}, u32[]{:S(2)}) async-start(f32[32,1,128]{2,1,0:T(1,128)} %bitcast.5), calls=%async_computation | async-start | bytes 32768 | tf_op jit(solution)/shard_map/all_to_all | solution.py:353
  73.6 1.5 copy-start.7
  75.1 1.5 copy-start.9
  76.6 1.5 copy-start.11
  78.1 4.2 %copy-start.2 = (f32[1,896,512]{2,1,0:T(8,128)S(1)}, f32[1,896,512]{2,1,0:T(8,128)}, u32[]{:S(2)}) copy-start(f32[1,896,512]{2,1,0:T(8,128)} %param.14) | copy-start | bytes 5505028
  78.1 4.2 %copy-start.3 = (f32[1,896,512]{2,1,0:T(8,128)S(1)}, f32[1,896,512]{2,1,0:T(8,128)}, u32[]{:S(2)}) copy-start(f32[1,896,512]{2,1,0:T(8,128)} %param.16) | copy-start | bytes 5505028
  78.1 4.2 %copy-start.5 = (f32[1,896,512]{2,1,0:T(8,128)S(1)}, f32[1,896,512]{2,1,0:T(8,128)}, u32[]{:S(2)}) copy-start(f32[1,896,512]{2,1,0:T(8,128)} %param.18) | copy-start | bytes 5505028
  78.6 1.2 copy-start.19
  79.8 1.2 copy-start.22
  81.1 1.2 copy-start.25
  82.9 1.2 copy-start.13
  84.1 1.2 copy-start.15
  85.3 1.2 copy-start.17
  86.5 1.5 copy-start.20
  88.0 1.5 copy-start.23
  89.5 1.5 copy-start.26
  91.0 1.3 copy-start.29
  92.4 3.1 %copy-start.14 = (f32[896,512]{1,0:T(8,128)S(1)}, f32[896,512]{1,0:T(8,128)}, u32[]{:S(2)}) copy-start(f32[896,512]{1,0:T(8,128)} %copy-done.13) | copy-start | bytes 5505028
  92.4 3.1 %copy-start.16 = (f32[896,512]{1,0:T(8,128)S(1)}, f32[896,512]{1,0:T(8,128)}, u32[]{:S(2)}) copy-start(f32[896,512]{1,0:T(8,128)} %copy-done.15) | copy-start | bytes 5505028
  92.4 3.1 %copy-start.18 = (f32[896,512]{1,0:T(8,128)S(1)}, f32[896,512]{1,0:T(8,128)}, u32[]{:S(2)}) copy-start(f32[896,512]{1,0:T(8,128)} %copy-done.17) | copy-start | bytes 5505028
  93.7 24.2 %collective-permute-start.14 = (bf16[384,896]{1,0:T(8,128)(2,1)S(1)}, bf16[384,896]{1,0:T(8,128)(2,1)S(1)}, u32[]{:S(2)}, u32[]{:S(2)}) collective-permute-start(bf16[384,896]{1,0:T(8,128)(2,1)S(1)} %shard_map.177.refs_1_), channel_id=1, source_target_pairs={{0,16},{8,24},{16,0},{24,8},{1,17},{9,25},{17,1},{25,9},{2,18},{10... | collective-permute-start | bytes 2064392 | tf_op jit(solution)/shard_map/ppermute | solution.py:327
  95.5 2.9 %copy-start.21 = (f32[512,896]{1,0:T(8,128)S(1)}, f32[512,896]{1,0:T(8,128)}, u32[]{:S(2)}) copy-start(f32[512,896]{1,0:T(8,128)} %copy-done.19) | copy-start | bytes 5505028
  95.5 2.9 %copy-start.24 = (f32[512,896]{1,0:T(8,128)S(1)}, f32[512,896]{1,0:T(8,128)}, u32[]{:S(2)}) copy-start(f32[512,896]{1,0:T(8,128)} %copy-done.22) | copy-start | bytes 5505028
  95.5 2.8 %copy-start.27 = (f32[512,896]{1,0:T(8,128)S(1)}, f32[512,896]{1,0:T(8,128)}, u32[]{:S(2)}) copy-start(f32[512,896]{1,0:T(8,128)} %copy-done.25) | copy-start | bytes 5505028
  95.5 2.8 %copy-start.32 = (f32[128,896]{1,0:T(8,128)S(1)}, f32[128,896]{1,0:T(8,128)}, u32[]{:S(2)}) copy-start(f32[128,896]{1,0:T(8,128)} %copy-done.31) | copy-start | bytes 1376260
  96.8 22.5 %collective-permute-start.9 = (bf16[672,512]{1,0:T(8,128)(2,1)S(1)}, bf16[672,512]{1,0:T(8,128)(2,1)S(1)}, u32[]{:S(2)}, u32[]{:S(2)}) collective-permute-start(bf16[672,512]{1,0:T(8,128)(2,1)S(1)} %shard_map.170.refs_1_), channel_id=1, source_target_pairs={{0,8},{8,0},{16,24},{24,16},{1,9},{9,1},{17,25},{25,17},{2,10},{10... | collective-permute-start | bytes 2064392 | tf_op jit(solution)/shard_map/ppermute | solution.py:327
  98.4 21.5 %copy-start.34 = (f32[224,512]{1,0:T(8,128)S(1)}, f32[224,512]{1,0:T(8,128)}, u32[]{:S(2)}) copy-start(f32[224,512]{1,0:T(8,128)} %copy-done.33) | copy-start | bytes 1376260
  98.8 17.4 %collective-permute-start.13 = (bf16[128,896]{1,0:T(8,128)(2,1)S(1)}, bf16[128,896]{1,0:T(8,128)(2,1)S(1)}, u32[]{:S(2)}, u32[]{:S(2)}) collective-permute-start(bf16[128,896]{1,0:T(8,128)(2,1)S(1)} %shard_map.176.refs_0_), channel_id=1, source_target_pairs={{0,16},{8,24},{16,0},{24,8},{1,17},{9,25},{17,1},{25,9},{2,18},{10... | collective-permute-start | bytes 688136 | tf_op jit(solution)/shard_map/ppermute | solution.py:327
  100.1 20.2 %collective-permute-start.15 = (bf16[128,896]{1,0:T(8,128)(2,1)S(1)}, bf16[128,896]{1,0:T(8,128)(2,1)S(1)}, u32[]{:S(2)}, u32[]{:S(2)}) collective-permute-start(bf16[128,896]{1,0:T(8,128)(2,1)S(1)} %shard_map.176.refs_0_), channel_id=1, source_target_pairs={{0,8},{8,0},{16,24},{24,16},{1,9},{9,1},{17,25},{25,17},{2,10},{10... | collective-permute-start | bytes 688136 | tf_op jit(solution)/shard_map/ppermute | solution.py:327
  101.4 60.0 %collective-permute-start.16 = (bf16[384,896]{1,0:T(8,128)(2,1)S(1)}, bf16[384,896]{1,0:T(8,128)(2,1)S(1)}, u32[]{:S(2)}, u32[]{:S(2)}) collective-permute-start(bf16[384,896]{1,0:T(8,128)(2,1)S(1)} %shard_map.177.refs_1_), channel_id=1, source_target_pairs={{0,8},{8,0},{16,24},{24,16},{1,9},{9,1},{17,25},{25,17},{2,10},{10... | collective-permute-start | bytes 2064392 | tf_op jit(solution)/shard_map/ppermute | solution.py:327
  116.2 64.2 %collective-permute-start.11 = (bf16[672,512]{1,0:T(8,128)(2,1)S(1)}, bf16[672,512]{1,0:T(8,128)(2,1)S(1)}, u32[]{:S(2)}, u32[]{:S(2)}) collective-permute-start(bf16[672,512]{1,0:T(8,128)(2,1)S(1)} %shard_map.170.refs_1_), channel_id=1, source_target_pairs={{0,16},{8,24},{16,0},{24,8},{1,17},{9,25},{17,1},{25,9},{2,18},{10... | collective-permute-start | bytes 2064392 | tf_op jit(solution)/shard_map/ppermute | solution.py:327
  117.9 64.1 %collective-permute-start.17 = (bf16[384,896]{1,0:T(8,128)(2,1)S(1)}, bf16[384,896]{1,0:T(8,128)(2,1)S(1)}, u32[]{:S(2)}, u32[]{:S(2)}) collective-permute-start(bf16[384,896]{1,0:T(8,128)(2,1)S(1)} %collective-permute-done.14.refs_2_), channel_id=1, source_target_pairs={{0,8},{8,0},{16,24},{24,16},{1,9},{9,1},{17,25},{25,17},{2,10},{10... | collective-permute-start | bytes 2064392 | tf_op jit(solution)/shard_map/ppermute | solution.py:327
  119.3 64.0 %collective-permute-start.12 = (bf16[672,512]{1,0:T(8,128)(2,1)S(1)}, bf16[672,512]{1,0:T(8,128)(2,1)S(1)}, u32[]{:S(2)}, u32[]{:S(2)}) collective-permute-start(bf16[672,512]{1,0:T(8,128)(2,1)S(1)} %collective-permute-done.9.refs_2_), channel_id=1, source_target_pairs={{0,16},{8,24},{16,0},{24,8},{1,17},{9,25},{17,1},{25,9},{2,18},{10... | collective-permute-start | bytes 2064392 | tf_op jit(solution)/shard_map/ppermute | solution.py:327
  120.3 33.1 %collective-permute-start.8 = (bf16[224,512]{1,0:T(8,128)(2,1)S(1)}, bf16[224,512]{1,0:T(8,128)(2,1)S(1)}, u32[]{:S(2)}, u32[]{:S(2)}) collective-permute-start(bf16[224,512]{1,0:T(8,128)(2,1)S(1)} %shard_map.169.refs_0_), channel_id=1, source_target_pairs={{0,8},{8,0},{16,24},{24,16},{1,9},{9,1},{17,25},{25,17},{2,10},{10... | collective-permute-start | bytes 688136 | tf_op jit(solution)/shard_map/ppermute | solution.py:327
  153.4 6.5 %collective-permute-start.10 = (bf16[224,512]{1,0:T(8,128)(2,1)S(1)}, bf16[224,512]{1,0:T(8,128)(2,1)S(1)}, u32[]{:S(2)}, u32[]{:S(2)}) collective-permute-start(bf16[224,512]{1,0:T(8,128)(2,1)S(1)} %shard_map.169.refs_0_), channel_id=1, source_target_pairs={{0,16},{8,24},{16,0},{24,8},{1,17},{9,25},{17,1},{25,9},{2,18},{10... | collective-permute-start | bytes 688136 | tf_op jit(solution)/shard_map/ppermute | solution.py:327
  159.9 24.8 %collective-permute-start.19 = (bf16[128,896]{1,0:T(8,128)(2,1)S(1)}, bf16[128,896]{1,0:T(8,128)(2,1)S(1)}, u32[]{:S(2)}, u32[]{:S(2)}) collective-permute-start(bf16[128,896]{1,0:T(8,128)(2,1)S(1)} %collective-permute-done.13.refs_1_), channel_id=1, source_target_pairs={{0,8},{8,0},{16,24},{24,16},{1,9},{9,1},{17,25},{25,17},{2,10},{10... | collective-permute-start | bytes 688136 | tf_op jit(solution)/shard_map/ppermute | solution.py:327
  161.4 23.3 %collective-permute-start.18 = (bf16[224,512]{1,0:T(8,128)(2,1)S(1)}, bf16[224,512]{1,0:T(8,128)(2,1)S(1)}, u32[]{:S(2)}, u32[]{:S(2)}) collective-permute-start(bf16[224,512]{1,0:T(8,128)(2,1)S(1)} %collective-permute-done.8.refs_1_), channel_id=1, source_target_pairs={{0,16},{8,24},{16,0},{24,8},{1,17},{9,25},{17,1},{25,9},{2,18},{10... | collective-permute-start | bytes 688136 | tf_op jit(solution)/shard_map/ppermute | solution.py:327
  164.6 1.7 copy-start.4
  164.7 2.4 %copy-start.6 = (f32[1,896,512]{2,1,0:T(8,128)S(1)}, f32[1,896,512]{2,1,0:T(8,128)}, u32[]{:S(2)}) copy-start(f32[1,896,512]{2,1,0:T(8,128)} %param.18) | copy-start | bytes 5505028
  167.0 4.0 %copy-start.8 = (f32[1,512,896]{2,1,0:T(8,128)S(1)}, f32[1,512,896]{2,1,0:T(8,128)}, u32[]{:S(2)}) copy-start(f32[1,512,896]{2,1,0:T(8,128)} %param.15) | copy-start | bytes 5505028
  167.0 4.0 %copy-start.10 = (f32[1,512,896]{2,1,0:T(8,128)S(1)}, f32[1,512,896]{2,1,0:T(8,128)}, u32[]{:S(2)}) copy-start(f32[1,512,896]{2,1,0:T(8,128)} %param.17) | copy-start | bytes 5505028
  167.0 4.6 %copy-start.12 = (f32[1,512,896]{2,1,0:T(8,128)S(1)}, f32[1,512,896]{2,1,0:T(8,128)}, u32[]{:S(2)}) copy-start(f32[1,512,896]{2,1,0:T(8,128)} %param.19) | copy-start | bytes 5505028
  167.0 4.9 %copy-start.30 = (f32[384,896]{1,0:T(8,128)S(1)}, f32[384,896]{1,0:T(8,128)}, u32[]{:S(2)}) copy-start(f32[384,896]{1,0:T(8,128)} %copy-done.28) | copy-start | bytes 4128772

commit v2 on v1

--- a/solution.py
+++ b/solution.py
@@ -57,10 +57,11 @@
 
         return pl.BlockSpec(self.block, index)
 
-    def quarter(self, ref, owner):
+    def quarter(self, ref, owner, start=0, blocks=BLOCKS):
+        first, size = start * self.step, blocks * self.step
         if self.axis == 0:
-            return ref.at[pl.ds(pl.multiple_of(owner * self.rows, self.rows), self.rows), :]
-        return ref.at[:, pl.ds(pl.multiple_of(owner * self.cols, self.cols), self.cols)]
+            return ref.at[pl.ds(pl.multiple_of(owner * self.rows + first, self.step), size), :]
+        return ref.at[pl.ds(first, size), pl.ds(pl.multiple_of(owner * self.cols, self.cols), self.cols)]
 
     def shard(self, start=0):
         return pl.BlockSpec(self.block, lambda i: (start + i, 0))
@@ -93,10 +94,10 @@
     )
 
 
-def cut_body(lays, partners, grads_one, grads_two, out_one, out_two, sems):
+def cut_body(lays, partners, start, blocks, grads_one, grads_two, out_one, out_two, sems):
     me = lax.axis_index("dp")
     copies = [
-        pltpu.make_async_copy(lay.quarter(grads, me ^ partner), out, sems.at[k])
+        pltpu.make_async_copy(lay.quarter(grads, me ^ partner, start, blocks), out, sems.at[k])
         for k, (lay, partner, grads, out) in enumerate(
             zip(lays, partners, (grads_one, grads_two), (out_one, out_two))
         )
@@ -107,13 +108,13 @@
         copy.wait()
 
 
-def cut(lays, grads, partners):
-    size = sum(lay.bytes(BLOCKS, 2) for lay in lays)
+def cut(lays, grads, partners, start=0, blocks=BLOCKS):
+    size = sum(lay.bytes(blocks, 2) for lay in lays)
     return pl.pallas_call(
-        functools.partial(cut_body, lays, partners),
+        functools.partial(cut_body, lays, partners, start, blocks),
         in_specs=[pl.BlockSpec(memory_space=pltpu.HBM)] * 2,
-        out_specs=[pl.BlockSpec(memory_space=pltpu.VMEM)] * 2,
-        out_shape=[pltpu.VMEM((lay.rows, lay.cols), jnp.bfloat16) for lay in lays],
+        out_specs=[pl.BlockSpec(memory_space=pl.ANY)] * 2,
+        out_shape=[pltpu.VMEM((blocks * lay.step, lay.cols), jnp.bfloat16) for lay in lays],
         scratch_shapes=[pltpu.SemaphoreType.DMA((2,))],
         compiler_params=pltpu.CompilerParams(vmem_limit_bytes=CUT_GRANT * 2**20),
         cost_estimate=pl.CostEstimate(flops=size, bytes_accessed=2 * size, transcendentals=0),
@@ -121,9 +122,10 @@
     )(*(pltpu.with_memory_space_constraint(g, pltpu.HBM) for g in grads))
 
 
-def add_body(grads, arrived, short, long):
-    value = (grads[...].astype(jnp.float32) + arrived[...].astype(jnp.float32)).astype(jnp.bfloat16)
+def add_body(grads, arrived_short, arrived_long, short, long):
     i = pl.program_id(0)
+    arrived = jnp.where(i < HEAD, arrived_short[...].astype(jnp.float32), arrived_long[...].astype(jnp.float32))
+    value = (grads[...].astype(jnp.float32) + arrived).astype(jnp.bfloat16)
 
     @pl.when(i < HEAD)
     def _():
@@ -134,15 +136,15 @@
         long[...] = value
 
 
-def add_forward(lay, grads, arrived, partner):
+def add_forward(lay, grads, short, long, partner):
     return call(
         add_body,
         BLOCKS,
-        [lay.piece(partner), lay.shard()],
+        [lay.piece(partner), lay.short(), lay.long()],
         [lay.short(), lay.long()],
         [lay.array(HEAD, jnp.bfloat16), lay.array(BLOCKS - HEAD, jnp.bfloat16)],
         lay.bytes(BLOCKS, 6),
-    )(grads, arrived)
+    )(grads, short, long)
 
 
 def partial_body(grads, arrived, accum, out):
@@ -239,15 +241,50 @@
     out[...] = shard_of(kept[...], pull[...], spread[...], scaled).astype(jnp.bfloat16)
 
 
-def weight_piece(lay, start, blocks, entries, sums, total, terms):
+def weight_tail(lay, entries, sums, total, terms):
+    n = BLOCKS - HEAD
     return call(
         functools.partial(weight_body, entries),
-        blocks,
-        [pl.BlockSpec(sums.shape, lambda i: (0, 0)), lay.shard()] + [lay.shard(start)] * 3,
+        n,
+        [pl.BlockSpec(sums.shape, lambda i: (0, 0)), lay.shard()] + [lay.shard(HEAD)] * 3,
         lay.shard(),
-        lay.array(blocks, jnp.bfloat16),
-        lay.bytes(blocks, 18),
+        lay.array(n, jnp.bfloat16),
+        lay.bytes(n, 18),
     )(sums, total, *terms)
+
+
+def weight_whole(lay, entries, sums, short, long, terms):
+    return call(
+        functools.partial(weight_whole_body, entries),
+        BLOCKS,
+        [pl.BlockSpec(sums.shape, lambda i: (0, 0)), lay.short(), lay.long()] + [lay.shard()] * 3,
+        lay.shard(),
+        lay.array(BLOCKS, jnp.bfloat16),
+        lay.bytes(BLOCKS, 22),
+    )(sums, short, long, *terms)
+
+
+def weight_whole_body(entries, sums, short, long, kept, pull, spread, out):
+    scaled = clip_of(entries, sums) * jnp.where(pl.program_id(0) < HEAD, short[...], long[...])
+    out[...] = shard_of(kept[...], pull[...], spread[...], scaled).astype(jnp.bfloat16)
+
+
+def weight_heads_body(entries, sums, *refs):
+    clip = clip_of(entries, sums)
+    for (total, kept, pull, spread), out in zip((refs[:4], refs[4:8]), refs[8:]):
+        out[...] = shard_of(kept[...], pull[...], spread[...], clip * total[...]).astype(jnp.bfloat16)
+
+
+def weight_heads(lays, entries, sums, totals, terms):
+    one, two = lays
+    return call(
+        functools.partial(weight_heads_body, entries),
+        HEAD,
+        [pl.BlockSpec(sums.shape, lambda i: (0, 0))] + [one.shard()] * 4 + [two.shard()] * 4,
+        [one.shard(), two.shard()],
+        [lay.array(HEAD, jnp.bfloat16) for lay in lays],
+        one.bytes(HEAD, 36),
+    )(sums, totals[0], *terms[0], totals[1], *terms[1])
 
 
 def update_body(entries, sums, short, long, master, moment, second, shard_out, first_out, variance_out):
@@ -270,22 +307,37 @@
     )(sums, short, long, *state)
 
 
-def place_body(*refs):
-    short, long, out = refs[-3:]
+def place_body(_, short, long, out):
     out[...] = jnp.where(pl.program_id(0) < HEAD, short[...], long[...])
 
 
 def place(lay, whole, short, long, partner):
+    return call(
+        place_body,
+        BLOCKS,
+        [pl.BlockSpec(memory_space=pl.ANY), lay.short(), lay.long()],
+        lay.piece(partner),
+        jax.ShapeDtypeStruct(lay.whole, jnp.bfloat16),
+        lay.bytes(BLOCKS, 4),
+        aliases={0: 0},
+    )(whole, short, long)
+
+
+def place_whole_body(*refs):
+    refs[-1][...] = refs[-2][...]
+
+
+def place_whole(lay, whole, piece, partner):
     first = whole is None
     return call(
-        place_body,
-        BLOCKS,
-        ([] if first else [pl.BlockSpec(memory_space=pl.ANY)]) + [lay.short(), lay.long()],
+        place_whole_body,
+        BLOCKS,
+        ([] if first else [pl.BlockSpec(memory_space=pl.ANY)]) + [lay.shard()],
         lay.piece(partner),
         jax.ShapeDtypeStruct(lay.whole, jnp.bfloat16),
         lay.bytes(BLOCKS, 4),
         aliases=None if first else {0: 0},
-    )(*([] if first else [whole]), short, long)
+    )(*([] if first else [whole]), piece)
 
 
 def place_long_body(_, long, out):
@@ -304,23 +356,31 @@
     )(whole, long)
 
 
-def place_short_body(_, __, one, two, out_one, out_two):
-    out_one[...] = one[...]
-    out_two[...] = two[...]
-
-
-def place_short(lays, wholes, shorts, partner):
-    one, two = lays
-    hbm = pl.BlockSpec(memory_space=pl.ANY)
-    return call(
-        place_short_body,
-        HEAD,
-        [hbm, hbm, one.shard(), two.shard()],
-        [one.piece(partner), two.piece(partner)],
-        [jax.ShapeDtypeStruct(lay.whole, jnp.bfloat16) for lay in lays],
-        one.bytes(HEAD, 8),
-        aliases={0: 0, 1: 1},
-    )(*wholes, *shorts)
+def place_heads_body(lays, partner, _, __, one, two, out_one, out_two, sems):
+    owner = lax.axis_index("dp") ^ partner
+    copies = []
+    for k, (lay, head, out) in enumerate(zip(lays, (one, two), (out_one, out_two))):
+        target = lay.quarter(out, owner, 0, HEAD)
+        copies.append(pltpu.make_async_copy(head, target, sems.at[k]))
+    for copy in copies:
+        copy.start()
+    for copy in copies:
+        copy.wait()
+
+
+def place_heads(lays, wholes, heads, partner):
+    size = sum(lay.bytes(HEAD, 2) for lay in lays)
+    return pl.pallas_call(
+        functools.partial(place_heads_body, lays, partner),
+        in_specs=[pl.BlockSpec(memory_space=pl.ANY)] * 4,
+        out_specs=[pl.BlockSpec(memory_space=pl.ANY)] * 2,
+        out_shape=[jax.ShapeDtypeStruct(lay.whole, jnp.bfloat16) for lay in lays],
+        scratch_shapes=[pltpu.SemaphoreType.DMA((2,))],
+        input_output_aliases={0: 0, 1: 1},
+        compiler_params=pltpu.CompilerParams(vmem_limit_bytes=CUT_GRANT * 2**20),
+        cost_estimate=pl.CostEstimate(flops=size, bytes_accessed=2 * size, transcendentals=0),
+        name="place_heads",
+    )(*wholes, *heads)
 
 
 def exchange(value, partner, parts):
@@ -341,9 +401,10 @@
     def move(values, partners):
         return [exchange(values[k], partners[k], parts) for k in both]
 
-    relayed = move(cut(lays, grads, (3, 3)), near)
+    relay_head = move(cut(lays, grads, (3, 3), 0, HEAD), near)
+    relay_tail = move(cut(lays, grads, (3, 3), HEAD, BLOCKS - HEAD), near)
     direct = move(cut(lays, grads, near), near)
-    sent = step(add_forward, grads, relayed, far)
+    sent = step(add_forward, grads, relay_head, relay_tail, far)
     tail = move([x[1] for x in sent], far)
     head = move([x[0] for x in sent], far)
     held = step(partial_sum, grads, direct, accums)
@@ -352,21 +413,19 @@
     head_totals, sums = short_squares(lays, held, head, sums, devices)
     sums = lax.all_to_all(sums, ("dp", "mp"), 0, 0, tiled=True)
 
-    def weights(start, blocks):
-        return lambda lay, total, terms: weight_piece(lay, start, blocks, entries, sums, total, terms)
-
-    own_head = step(weights(0, HEAD), head_totals, terms)
-    own_tail = step(weights(HEAD, BLOCKS - HEAD), tail_totals, terms)
+    own_head = weight_heads(lays, entries, sums, head_totals, terms)
+    own_tail = step(lambda lay, *x: weight_tail(lay, entries, sums, *x), tail_totals, terms)
     near_head, near_tail = move(own_head, near), move(own_tail, near)
-    far_tail, far_head = move(own_tail, far), move(own_head, far)
+    own = step(lambda lay, *x: weight_whole(lay, entries, sums, *x), head_totals, tail_totals, terms)
+    opposite = move(own, far)
     last_tail, last_head = move(near_tail, far), move(near_head, far)
 
     updated = step(lambda lay, *x: update(lay, entries, sums, *x), head_totals, tail_totals, states)
-    wholes = step(place, (None, None), own_head, own_tail, (0, 0))
+    wholes = step(place_whole, (None, None), own, (0, 0))
     wholes = step(place, wholes, near_head, near_tail, near)
-    wholes = step(place, wholes, far_head, far_tail, far)
+    wholes = step(place_whole, wholes, opposite, far)
     wholes = step(place_long, wholes, last_tail, (3, 3))
-    wholes = place_short(lays, wholes, last_head, 3)
+    wholes = place_heads(lays, wholes, last_head, 3)
     return tuple(w[None] for w in wholes) + tuple(updated[k][j][None] for j in range(3) for k in both)
 
 

time: 186 us -> 184 us (0.989)
  Pallas kernels: 31.2 us -> 35.8 us
  waiting for transfers between devices: 97.4 us -> 92.9 us
    pallas_call x15 -> x17, Pallas kernels: 17.3 us -> 22 us  [the longest x4 5.93 us: place_whole(): call(place_whole_body, BLOCKS, ([] if first else [pl.BlockSpec(memory_spa...]
    ppermute x20, waiting for transfers between devices: 97.4 us -> 92.9 us  [exchange(): return lax.ppermute(value, 'dp', [(i, i ^ partner) for i in range(parts)])]
    unnamed x74 -> x70, local copies, waits for them, and re-layouts: 23.4 us -> 21.7 us
  transfers between devices with their start and end apart: 21 -> 21, of which waited for: 7 -> 9; matrix products, arithmetic and copies ran while one was open for 0% -> 0% of each run, Pallas kernels for 14% -> 17%
where the time goes in v2:
time: 184 us; the launch traced here: 183 us
  waiting for transfers between devices  92.9 us (50%)
  Pallas kernels  35.8 us (19%)
  starting transfers between devices  31.8 us (17%)
  local copies, waits for them, and re-layouts  21.7 us (12%)
    ppermute x20, waiting for transfers between devices, exchange(): return lax.ppermute(value, 'dp', [(i, i ^ partner) for i in range(parts)])  92.9 us
    ppermute x20, starting transfers between devices, exchange(): return lax.ppermute(value, 'dp', [(i, i ^ partner) for i in range(parts)])  26.9 us
    unnamed x70, local copies, waits for them, and re-layouts  21.7 us
    pallas_call x2, Pallas kernels, update(): call(functools.partial(update_body, entries), BLOCKS, [pl.BlockSpec(sums....  7.9 us
    pallas_call x4, Pallas kernels, place_whole(): call(place_whole_body, BLOCKS, ([] if first else [pl.BlockSpec(memory_spa...  5.93 us
    all_to_all x1, starting transfers between devices, on_square(): sums = lax.all_to_all(sums, ('dp', 'mp'), 0, 0, tiled=True)  4.92 us
    pallas_call x3, Pallas kernels, cut(): pl.pallas_call(functools.partial(cut_body, lays, partners, start, blocks)...  4.02 us
  transfers between devices with their start and end apart: 21, of which 9 were waited for; matrix products, arithmetic and copies ran while one was open for 0% of the time, Pallas kernels for 17%

profile of v2, /device:TPU:0, one launch (start us, length us, event | category | flops | bytes accessed | tf_op | source)
XLA Modules:
  0.0 183.1 jit_solution(8231807694973815895)
XLA Ops:
  0.6 1.3 cut.5
  2.0 3.0 %collective-permute-start.2 = (bf16[672,512]{1,0:T(8,128)(2,1)S(1)}, bf16[672,512]{1,0:T(8,128)(2,1)S(1)}, u32[]{:S(2)}, u32[]{:S(2)}) collective-permute-start(bf16[672,512]{1,0:T(8,128)(2,1)S(1)} %get-tuple-element.43), channel_id=1, source_target_pairs={{0,8},{8,0},{16,24},{24,16},{1,9},{9,1},{17,25},{25,17},{2,10},{10... | collective-permute-start | bytes 2064392 | tf_op jit(solution)/shard_map/ppermute | solution.py:387
  5.0 1.5 collective-permute-start.6
  6.5 1.1 cut.4
  8.2 1.6 cut.3
  9.8 1.6 collective-permute-start
  11.9 14.3 %collective-permute-done.1.arrived_short = bf16[224,512]{1,0:T(8,128)(2,1)S(1)} collective-permute-done((bf16[224,512]{1,0:T(8,128)(2,1)S(1)}, bf16[224,512]{1,0:T(8,128)(2,1)S(1)}, u32[]{:S(2)}, u32[]{:S(2)}) %collective-permute-start.1) | collective-permute-done | bytes 229408 | tf_op jit(solution)/shard_map/ppermute | solution.py:387
  26.2 2.0 %collective-permute-start.5 = (bf16[128,896]{1,0:T(8,128)(2,1)S(1)}, bf16[128,896]{1,0:T(8,128)(2,1)S(1)}, u32[]{:S(2)}, u32[]{:S(2)}) collective-permute-start(bf16[128,896]{1,0:T(8,128)(2,1)S(1)} %get-tuple-element.46), channel_id=1, source_target_pairs={{0,16},{8,24},{16,0},{24,8},{1,17},{9,25},{17,1},{25,9},{2,18},{10... | collective-permute-start | bytes 688136 | tf_op jit(solution)/shard_map/ppermute | solution.py:387
  29.0 18.9 %collective-permute-done.5.arrived_short = bf16[128,896]{1,0:T(8,128)(2,1)S(1)} collective-permute-done((bf16[128,896]{1,0:T(8,128)(2,1)S(1)}, bf16[128,896]{1,0:T(8,128)(2,1)S(1)}, u32[]{:S(2)}, u32[]{:S(2)}) %collective-permute-start.5) | collective-permute-done | bytes 229408 | tf_op jit(solution)/shard_map/ppermute | solution.py:387
  47.9 0.8 shard_map.164
  48.8 2.0 %collective-permute-start.3 = (bf16[224,512]{1,0:T(8,128)(2,1)S(1)}, bf16[224,512]{1,0:T(8,128)(2,1)S(1)}, u32[]{:S(2)}, u32[]{:S(2)}) collective-permute-start(bf16[224,512]{1,0:T(8,128)(2,1)S(1)} %get-tuple-element.44), channel_id=1, source_target_pairs={{0,16},{8,24},{16,0},{24,8},{1,17},{9,25},{17,1},{25,9},{2,18},{10... | collective-permute-start | bytes 688136 | tf_op jit(solution)/shard_map/ppermute | solution.py:387
  50.8 1.5 collective-permute-start.7
  52.7 1.2 copy-done.34
  54.3 8.4 %collective-permute-done.8.arrived = bf16[672,512]{1,0:T(8,128)(2,1)S(1)} collective-permute-done((bf16[672,512]{1,0:T(8,128)(2,1)S(1)}, bf16[672,512]{1,0:T(8,128)(2,1)S(1)}, u32[]{:S(2)}, u32[]{:S(2)}) %collective-permute-start.8) | collective-permute-done | bytes 688160 | tf_op jit(solution)/shard_map/ppermute | solution.py:387
  62.9 3.0 %collective-permute-done.9.arrived = bf16[384,896]{1,0:T(8,128)(2,1)S(1)} collective-permute-done((bf16[384,896]{1,0:T(8,128)(2,1)S(1)}, bf16[384,896]{1,0:T(8,128)(2,1)S(1)}, u32[]{:S(2)}, u32[]{:S(2)}) %collective-permute-start.9) | collective-permute-done | bytes 688160 | tf_op jit(solution)/shard_map/ppermute | solution.py:387
  66.1 1.1 copy-done.14
  67.2 1.1 collective-permute-done.7.arrived_two
  68.3 0.8 shard_map.167
  69.1 0.8 copy-done.29
  69.9 0.8 copy-done.31
  70.6 4.9 %all-to-all-start = ((f32[32,1,128]{2,1,0:T(1,128)}), f32[32,1,128]{2,1,0:T(1,128)S(1)}, u32[]{:S(2)}, u32[]{:S(2)}) async-start(f32[32,1,128]{2,1,0:T(1,128)} %bitcast.5), calls=%async_computation | async-start | bytes 32768 | tf_op jit(solution)/shard_map/all_to_all | solution.py:414
  75.6 1.5 copy-done.23
  77.1 1.5 copy-done.25
  78.6 1.5 copy-done.27
  80.6 1.2 copy-done.2
  81.9 1.2 copy-done.5
  83.1 0.9 copy-done.21
  84.6 1.2 copy-done.8
  85.8 1.2 copy-done.10
  87.0 1.2 copy-done.12
  88.2 1.5 copy-done.3
  89.7 1.5 copy-done.6
  91.2 1.3 copy-done.15
  92.6 1.3 shard_map.179
  93.9 1.8 %collective-permute-start.15 = (bf16[384,896]{1,0:T(8,128)(2,1)S(1)}, bf16[384,896]{1,0:T(8,128)(2,1)S(1)}, u32[]{:S(2)}, u32[]{:S(2)}) collective-permute-start(bf16[384,896]{1,0:T(8,128)(2,1)S(1)} %shard_map.179), channel_id=1, source_target_pairs={{0,16},{8,24},{16,0},{24,8},{1,17},{9,25},{17,1},{25,9},{2,18},{10... | collective-permute-start | bytes 2064392 | tf_op jit(solution)/shard_map/ppermute | solution.py:387
  95.7 1.3 shard_map.173
  97.0 1.5 collective-permute-start.11
  98.6 1.8 shard_map.177.refs_0_
  100.4 0.8 collective-permute-start.16
  101.2 1.8 shard_map.169.refs_0_
  103.0 1.3 collective-permute-start.12
  104.3 8.0 %collective-permute-done.15.long = bf16[384,896]{1,0:T(8,128)(2,1)S(1)} collective-permute-done((bf16[384,896]{1,0:T(8,128)(2,1)S(1)}, bf16[384,896]{1,0:T(8,128)(2,1)S(1)}, u32[]{:S(2)}, u32[]{:S(2)}) %collective-permute-start.15) | collective-permute-done | bytes 688160 | tf_op jit(solution)/shard_map/ppermute | solution.py:387
  112.2 1.8 collective-permute-start.17
  114.0 1.4 collective-permute-done.11.long
  115.4 1.2 collective-permute-start.13
  116.6 0.7 shard_map.172
  117.3 0.9 collective-permute-start.14
  118.2 32.6 %collective-permute-done.14.short = bf16[128,896]{1,0:T(8,128)(2,1)S(1)} collective-permute-done((bf16[128,896]{1,0:T(8,128)(2,1)S(1)}, bf16[128,896]{1,0:T(8,128)(2,1)S(1)}, u32[]{:S(2)}, u32[]{:S(2)}) %collective-permute-start.14) | collective-permute-done | bytes 229408 | tf_op jit(solution)/shard_map/ppermute | solution.py:387
  150.8 1.6 collective-permute-start.10
  152.5 5.3 %collective-permute-done.10.short = bf16[224,512]{1,0:T(8,128)(2,1)S(1)} collective-permute-done((bf16[224,512]{1,0:T(8,128)(2,1)S(1)}, bf16[224,512]{1,0:T(8,128)(2,1)S(1)}, u32[]{:S(2)}, u32[]{:S(2)}) %collective-permute-start.10) | collective-permute-done | bytes 229408 | tf_op jit(solution)/shard_map/ppermute | solution.py:387
  157.7 1.5 collective-permute-start.18
  159.2 1.5 collective-permute-start.19
  160.7 1.5 shard_map.178._
  162.2 1.5 shard_map.170._
  163.9 0.7 copy-done.20
  164.6 4.0 %shard_map.183 = (f32[896,512]{1,0:T(8,128)}, f32[896,512]{1,0:T(8,128)}, f32[896,512]{1,0:T(8,128)}) custom-call(f32[32,128]{1,0:T(8,128)S(1)} %bitcast.51, f32[224,512]{1,0:T(8,128)S(1)} %copy-done.32, f32[672,512]{1,0:T(8,128)S(1)} %get-tuple-element.55.long.total, f32[896,512]{1,0:T(8,128)S(1)} %bitcast.33, f32[896,512]{1,0:T(8,128)S(1)} %bitcast.35, ...), custom_call_target="tpu_custom_call" | custom-call | flops 25690112 | bytes 12845056 | tf_op jit(solution)/shard_map/pallas_call | solution.py:300
  169.6 3.9 %shard_map.184 = (f32[512,896]{1,0:T(8,128)}, f32[512,896]{1,0:T(8,128)}, f32[512,896]{1,0:T(8,128)}) custom-call(f32[32,128]{1,0:T(8,128)S(1)} %bitcast.52, f32[128,896]{1,0:T(8,128)S(1)} %copy-done.30, f32[384,896]{1,0:T(8,128)S(1)} %copy-done.16, f32[512,896]{1,0:T(8,128)S(1)} %bitcast.39, f32[512,896]{1,0:T(8,128)S(1)} %bitcast.41, f32[512,896]{1,0:T(8,128)S(1)} %bitcast.43), custom_call_target="tpu_custom_call" | custom-call | flops 25690112 | bytes 12845056 | tf_op jit(solution)/shard_map/pallas_call | solution.py:300
  173.5 1.5 shard_map.180.refs_0_
  175.0 1.5 shard_map.174.refs_0_
  176.5 1.5 shard_map.181._
  178.0 1.5 shard_map.175._
  179.5 1.4 shard_map.182.__
  180.9 1.4 shard_map.176._
  182.3 0.8 place_heads.1
  (76 shorter events, 5.6 us)
Async XLA Ops:
  2.0 26.3 %collective-permute-start.2 = (bf16[672,512]{1,0:T(8,128)(2,1)S(1)}, bf16[672,512]{1,0:T(8,128)(2,1)S(1)}, u32[]{:S(2)}, u32[]{:S(2)}) collective-permute-start(bf16[672,512]{1,0:T(8,128)(2,1)S(1)} %get-tuple-element.43), channel_id=1, source_target_pairs={{0,8},{8,0},{16,24},{24,16},{1,9},{9,1},{17,25},{25,17},{2,10},{10... | collective-permute-start | bytes 2064392 | tf_op jit(solution)/shard_map/ppermute | solution.py:387
  5.0 42.9 %collective-permute-start.6 = (bf16[384,896]{1,0:T(8,128)(2,1)S(1)}, bf16[384,896]{1,0:T(8,128)(2,1)S(1)}, u32[]{:S(2)}, u32[]{:S(2)}) collective-permute-start(bf16[384,896]{1,0:T(8,128)(2,1)S(1)} %get-tuple-element.47), channel_id=1, source_target_pairs={{0,16},{8,24},{16,0},{24,8},{1,17},{9,25},{17,1},{25,9},{2,18},{10... | collective-permute-start | bytes 2064392 | tf_op jit(solution)/shard_map/ppermute | solution.py:387
  7.6 18.6 %collective-permute-start.1 = (bf16[224,512]{1,0:T(8,128)(2,1)S(1)}, bf16[224,512]{1,0:T(8,128)(2,1)S(1)}, u32[]{:S(2)}, u32[]{:S(2)}) collective-permute-start(bf16[224,512]{1,0:T(8,128)(2,1)S(1)} %get-tuple-element.42), channel_id=1, source_target_pairs={{0,8},{8,0},{16,24},{24,16},{1,9},{9,1},{17,25},{25,17},{2,10},{10... | collective-permute-start | bytes 688136 | tf_op jit(solution)/shard_map/ppermute | solution.py:387
  8.2 20.1 %copy-start = (bf16[1,1,3584,512]{3,2,1,0:T(8,128)(2,1)S(1)}, bf16[1,1,3584,512]{3,2,1,0:T(8,128)(2,1)}, u32[]{:S(2)}) copy-start(bf16[1,1,3584,512]{3,2,1,0:T(8,128)(2,1)} %param.10) | copy-start | bytes 11010052
  9.8 41.0 %collective-permute-start = (bf16[896,512]{1,0:T(8,128)(2,1)S(1)}, bf16[896,512]{1,0:T(8,128)(2,1)S(1)}, u32[]{:S(2)}, u32[]{:S(2)}) collective-permute-start(bf16[896,512]{1,0:T(8,128)(2,1)S(1)} %get-tuple-element.41), channel_id=1, source_target_pairs={{0,8},{8,0},{16,24},{24,16},{1,9},{9,1},{17,25},{25,17},{2,10},{10... | collective-permute-start | bytes 2752520 | tf_op jit(solution)/shard_map/ppermute | solution.py:387
  11.4 41.3 %collective-permute-start.4 = (bf16[512,896]{1,0:T(8,128)(2,1)S(1)}, bf16[512,896]{1,0:T(8,128)(2,1)S(1)}, u32[]{:S(2)}, u32[]{:S(2)}) collective-permute-start(bf16[512,896]{1,0:T(8,128)(2,1)S(1)} %get-tuple-element.45), channel_id=1, source_target_pairs={{0,16},{8,24},{16,0},{24,8},{1,17},{9,25},{17,1},{25,9},{2,18},{10... | collective-permute-start | bytes 2752520 | tf_op jit(solution)/shard_map/ppermute | solution.py:387
  26.2 21.7 %copy-start.1 = (bf16[1,1,512,3584]{3,2,1,0:T(8,128)(2,1)S(1)}, bf16[1,1,512,3584]{3,2,1,0:T(8,128)(2,1)}, u32[]{:S(2)}) copy-start(bf16[1,1,512,3584]{3,2,1,0:T(8,128)(2,1)} %param.11) | copy-start | bytes 11010052
  26.2 21.7 %collective-permute-start.5 = (bf16[128,896]{1,0:T(8,128)(2,1)S(1)}, bf16[128,896]{1,0:T(8,128)(2,1)S(1)}, u32[]{:S(2)}, u32[]{:S(2)}) collective-permute-start(bf16[128,896]{1,0:T(8,128)(2,1)S(1)} %get-tuple-element.46), channel_id=1, source_target_pairs={{0,16},{8,24},{16,0},{24,8},{1,17},{9,25},{17,1},{25,9},{2,18},{10... | collective-permute-start | bytes 688136 | tf_op jit(solution)/shard_map/ppermute | solution.py:387
  28.9 23.4 %copy-start.33 = (f32[1,896,512]{2,1,0:T(8,128)S(1)}, f32[1,896,512]{2,1,0:T(8,128)}, u32[]{:S(2)}) copy-start(f32[1,896,512]{2,1,0:T(8,128)} %param.12) | copy-start | bytes 5505028
  28.9 33.8 %collective-permute-start.8 = (bf16[672,512]{1,0:T(8,128)(2,1)S(1)}, bf16[672,512]{1,0:T(8,128)(2,1)S(1)}, u32[]{:S(2)}, u32[]{:S(2)}) collective-permute-start(bf16[672,512]{1,0:T(8,128)(2,1)S(1)} %get-tuple-element.49), channel_id=1, source_target_pairs={{0,16},{8,24},{16,0},{24,8},{1,17},{9,25},{17,1},{25,9},{2,18},{10... | collective-permute-start | bytes 2064392 | tf_op jit(solution)/shard_map/ppermute | solution.py:387
  48.7 17.2 %collective-permute-start.9 = (bf16[384,896]{1,0:T(8,128)(2,1)S(1)}, bf16[384,896]{1,0:T(8,128)(2,1)S(1)}, u32[]{:S(2)}, u32[]{:S(2)}) collective-permute-start(bf16[384,896]{1,0:T(8,128)(2,1)S(1)} %get-tuple-element.51), channel_id=1, source_target_pairs={{0,8},{8,0},{16,24},{24,16},{1,9},{9,1},{17,25},{25,17},{2,10},{10... | collective-permute-start | bytes 2064392 | tf_op jit(solution)/shard_map/ppermute | solution.py:387
  48.8 18.4 %collective-permute-start.3 = (bf16[224,512]{1,0:T(8,128)(2,1)S(1)}, bf16[224,512]{1,0:T(8,128)(2,1)S(1)}, u32[]{:S(2)}, u32[]{:S(2)}) collective-permute-start(bf16[224,512]{1,0:T(8,128)(2,1)S(1)} %get-tuple-element.44), channel_id=1, source_target_pairs={{0,16},{8,24},{16,0},{24,8},{1,17},{9,25},{17,1},{25,9},{2,18},{10... | collective-permute-start | bytes 688136 | tf_op jit(solution)/shard_map/ppermute | solution.py:387
  50.8 17.5 %collective-permute-start.7 = (bf16[128,896]{1,0:T(8,128)(2,1)S(1)}, bf16[128,896]{1,0:T(8,128)(2,1)S(1)}, u32[]{:S(2)}, u32[]{:S(2)}) collective-permute-start(bf16[128,896]{1,0:T(8,128)(2,1)S(1)} %get-tuple-element.48), channel_id=1, source_target_pairs={{0,8},{8,0},{16,24},{24,16},{1,9},{9,1},{17,25},{25,17},{2,10},{10... | collective-permute-start | bytes 688136 | tf_op jit(solution)/shard_map/ppermute | solution.py:387
  52.3 1.5 copy-start.34
  66.1 1.1 copy-start.14
  69.1 0.8 copy-start.29
  69.9 0.8 copy-start.31
  70.6 17.6 %all-to-all-start = ((f32[32,1,128]{2,1,0:T(1,128)}), f32[32,1,128]{2,1,0:T(1,128)S(1)}, u32[]{:S(2)}, u32[]{:S(2)}) async-start(f32[32,1,128]{2,1,0:T(1,128)} %bitcast.5), calls=%async_computation | async-start | bytes 32768 | tf_op jit(solution)/shard_map/all_to_all | solution.py:414
  75.6 1.5 copy-start.23
  77.1 1.5 copy-start.25
  78.6 1.5 copy-start.27
  80.1 3.0 %copy-start.17 = (f32[1,896,512]{2,1,0:T(8,128)S(1)}, f32[1,896,512]{2,1,0:T(8,128)}, u32[]{:S(2)}) copy-start(f32[1,896,512]{2,1,0:T(8,128)} %param.14) | copy-start | bytes 5505028
  80.1 3.0 %copy-start.19 = (f32[1,896,512]{2,1,0:T(8,128)S(1)}, f32[1,896,512]{2,1,0:T(8,128)}, u32[]{:S(2)}) copy-start(f32[1,896,512]{2,1,0:T(8,128)} %param.16) | copy-start | bytes 5505028
  80.1 3.9 %copy-start.21 = (f32[1,896,512]{2,1,0:T(8,128)S(1)}, f32[1,896,512]{2,1,0:T(8,128)}, u32[]{:S(2)}) copy-start(f32[1,896,512]{2,1,0:T(8,128)} %param.18) | copy-start | bytes 5505028
  80.6 1.2 copy-start.2
  81.9 1.2 copy-start.5
  84.5 1.2 copy-start.8
  85.8 1.2 copy-start.10
  87.0 1.2 copy-start.12
  88.2 1.5 copy-start.3
  89.7 1.5 copy-start.6
  91.2 1.3 copy-start.15
  92.6 3.1 %copy-start.9 = (f32[896,512]{1,0:T(8,128)S(1)}, f32[896,512]{1,0:T(8,128)}, u32[]{:S(2)}) copy-start(f32[896,512]{1,0:T(8,128)} %copy-done.8) | copy-start | bytes 5505028
  92.6 3.1 %copy-start.11 = (f32[896,512]{1,0:T(8,128)S(1)}, f32[896,512]{1,0:T(8,128)}, u32[]{:S(2)}) copy-start(f32[896,512]{1,0:T(8,128)} %copy-done.10) | copy-start | bytes 5505028
  92.6 3.1 %copy-start.13 = (f32[896,512]{1,0:T(8,128)S(1)}, f32[896,512]{1,0:T(8,128)}, u32[]{:S(2)}) copy-start(f32[896,512]{1,0:T(8,128)} %copy-done.12) | copy-start | bytes 5505028
  93.9 18.4 %collective-permute-start.15 = (bf16[384,896]{1,0:T(8,128)(2,1)S(1)}, bf16[384,896]{1,0:T(8,128)(2,1)S(1)}, u32[]{:S(2)}, u32[]{:S(2)}) collective-permute-start(bf16[384,896]{1,0:T(8,128)(2,1)S(1)} %shard_map.179), channel_id=1, source_target_pairs={{0,16},{8,24},{16,0},{24,8},{1,17},{9,25},{17,1},{25,9},{2,18},{10... | collective-permute-start | bytes 2064392 | tf_op jit(solution)/shard_map/ppermute | solution.py:387
  95.7 2.8 %copy-start.4 = (f32[512,896]{1,0:T(8,128)S(1)}, f32[512,896]{1,0:T(8,128)}, u32[]{:S(2)}) copy-start(f32[512,896]{1,0:T(8,128)} %copy-done.2) | copy-start | bytes 5505028
  95.7 2.8 %copy-start.7 = (f32[512,896]{1,0:T(8,128)S(1)}, f32[512,896]{1,0:T(8,128)}, u32[]{:S(2)}) copy-start(f32[512,896]{1,0:T(8,128)} %copy-done.5) | copy-start | bytes 5505028
  95.7 2.8 %copy-start.30 = (f32[128,896]{1,0:T(8,128)S(1)}, f32[128,896]{1,0:T(8,128)}, u32[]{:S(2)}) copy-start(f32[128,896]{1,0:T(8,128)} %copy-done.29) | copy-start | bytes 1376260
  97.0 18.4 %collective-permute-start.11 = (bf16[672,512]{1,0:T(8,128)(2,1)S(1)}, bf16[672,512]{1,0:T(8,128)(2,1)S(1)}, u32[]{:S(2)}, u32[]{:S(2)}) collective-permute-start(bf16[672,512]{1,0:T(8,128)(2,1)S(1)} %shard_map.173), channel_id=1, source_target_pairs={{0,8},{8,0},{16,24},{24,16},{1,9},{9,1},{17,25},{25,17},{2,10},{10... | collective-permute-start | bytes 2064392 | tf_op jit(solution)/shard_map/ppermute | solution.py:387
  98.5 2.6 %copy-start.32 = (f32[224,512]{1,0:T(8,128)S(1)}, f32[224,512]{1,0:T(8,128)}, u32[]{:S(2)}) copy-start(f32[224,512]{1,0:T(8,128)} %copy-done.31) | copy-start | bytes 1376260
  100.4 58.9 %collective-permute-start.16 = (bf16[512,896]{1,0:T(8,128)(2,1)S(1)}, bf16[512,896]{1,0:T(8,128)(2,1)S(1)}, u32[]{:S(2)}, u32[]{:S(2)}) collective-permute-start(bf16[512,896]{1,0:T(8,128)(2,1)S(1)} %shard_map.177.refs_0_), channel_id=1, source_target_pairs={{0,8},{8,0},{16,24},{24,16},{1,9},{9,1},{17,25},{25,17},{2,10},{10... | collective-permute-start | bytes 2752520 | tf_op jit(solution)/shard_map/ppermute | solution.py:387
  103.0 75.1 %collective-permute-start.12 = (bf16[896,512]{1,0:T(8,128)(2,1)S(1)}, bf16[896,512]{1,0:T(8,128)(2,1)S(1)}, u32[]{:S(2)}, u32[]{:S(2)}) collective-permute-start(bf16[896,512]{1,0:T(8,128)(2,1)S(1)} %shard_map.169.refs_0_), channel_id=1, source_target_pairs={{0,16},{8,24},{16,0},{24,8},{1,17},{9,25},{17,1},{25,9},{2,18},{10... | collective-permute-start | bytes 2752520 | tf_op jit(solution)/shard_map/ppermute | solution.py:387
  112.2 67.3 %collective-permute-start.17 = (bf16[384,896]{1,0:T(8,128)(2,1)S(1)}, bf16[384,896]{1,0:T(8,128)(2,1)S(1)}, u32[]{:S(2)}, u32[]{:S(2)}) collective-permute-start(bf16[384,896]{1,0:T(8,128)(2,1)S(1)} %collective-permute-done.15.long), channel_id=1, source_target_pairs={{0,8},{8,0},{16,24},{24,16},{1,9},{9,1},{17,25},{25,17},{2,10},{10... | collective-permute-start | bytes 2064392 | tf_op jit(solution)/shard_map/ppermute | solution.py:387
  115.4 65.5 %collective-permute-start.13 = (bf16[672,512]{1,0:T(8,128)(2,1)S(1)}, bf16[672,512]{1,0:T(8,128)(2,1)S(1)}, u32[]{:S(2)}, u32[]{:S(2)}) collective-permute-start(bf16[672,512]{1,0:T(8,128)(2,1)S(1)} %collective-permute-done.11.long), channel_id=1, source_target_pairs={{0,16},{8,24},{16,0},{24,8},{1,17},{9,25},{17,1},{25,9},{2,18},{10... | collective-permute-start | bytes 2064392 | tf_op jit(solution)/shard_map/ppermute | solution.py:387
  117.3 33.5 %collective-permute-start.14 = (bf16[128,896]{1,0:T(8,128)(2,1)S(1)}, bf16[128,896]{1,0:T(8,128)(2,1)S(1)}, u32[]{:S(2)}, u32[]{:S(2)}) collective-permute-start(bf16[128,896]{1,0:T(8,128)(2,1)S(1)} %get-tuple-element.65), channel_id=1, source_target_pairs={{0,16},{8,24},{16,0},{24,8},{1,17},{9,25},{17,1},{25,9},{2,18},{10... | collective-permute-start | bytes 688136 | tf_op jit(solution)/shard_map/ppermute | solution.py:387
  150.8 6.9 %collective-permute-start.10 = (bf16[224,512]{1,0:T(8,128)(2,1)S(1)}, bf16[224,512]{1,0:T(8,128)(2,1)S(1)}, u32[]{:S(2)}, u32[]{:S(2)}) collective-permute-start(bf16[224,512]{1,0:T(8,128)(2,1)S(1)} %get-tuple-element.63), channel_id=1, source_target_pairs={{0,8},{8,0},{16,24},{24,16},{1,9},{9,1},{17,25},{25,17},{2,10},{10... | collective-permute-start | bytes 688136 | tf_op jit(solution)/shard_map/ppermute | solution.py:387
  157.7 24.6 %collective-permute-start.18 = (bf16[224,512]{1,0:T(8,128)(2,1)S(1)}, bf16[224,512]{1,0:T(8,128)(2,1)S(1)}, u32[]{:S(2)}, u32[]{:S(2)}) collective-permute-start(bf16[224,512]{1,0:T(8,128)(2,1)S(1)} %collective-permute-done.10.short), channel_id=1, source_target_pairs={{0,16},{8,24},{16,0},{24,8},{1,17},{9,25},{17,1},{25,9},{2,18},{10... | collective-permute-start | bytes 688136 | tf_op jit(solution)/shard_map/ppermute | solution.py:387
  159.2 23.1 %collective-permute-start.19 = (bf16[128,896]{1,0:T(8,128)(2,1)S(1)}, bf16[128,896]{1,0:T(8,128)(2,1)S(1)}, u32[]{:S(2)}, u32[]{:S(2)}) collective-permute-start(bf16[128,896]{1,0:T(8,128)(2,1)S(1)} %collective-permute-done.14.short), channel_id=1, source_target_pairs={{0,8},{8,0},{16,24},{24,16},{1,9},{9,1},{17,25},{25,17},{2,10},{10... | collective-permute-start | bytes 688136 | tf_op jit(solution)/shard_map/ppermute | solution.py:387
  160.7 3.0 %copy-start.22 = (f32[1,896,512]{2,1,0:T(8,128)S(1)}, f32[1,896,512]{2,1,0:T(8,128)}, u32[]{:S(2)}) copy-start(f32[1,896,512]{2,1,0:T(8,128)} %param.18) | copy-start | bytes 5505028
  162.2 1.7 copy-start.18
  162.2 2.4 %copy-start.20 = (f32[1,896,512]{2,1,0:T(8,128)S(1)}, f32[1,896,512]{2,1,0:T(8,128)}, u32[]{:S(2)}) copy-start(f32[1,896,512]{2,1,0:T(8,128)} %param.16) | copy-start | bytes 5505028
  164.6 4.0 %copy-start.16 = (f32[384,896]{1,0:T(8,128)S(1)}, f32[384,896]{1,0:T(8,128)}, u32[]{:S(2)}) copy-start(f32[384,896]{1,0:T(8,128)} %copy-done.14) | copy-start | bytes 4128772
  164.6 4.0 %copy-start.24 = (f32[1,512,896]{2,1,0:T(8,128)S(1)}, f32[1,512,896]{2,1,0:T(8,128)}, u32[]{:S(2)}) copy-start(f32[1,512,896]{2,1,0:T(8,128)} %param.15) | copy-start | bytes 5505028
  164.6 4.3 %copy-start.26 = (f32[1,512,896]{2,1,0:T(8,128)S(1)}, f32[1,512,896]{2,1,0:T(8,128)}, u32[]{:S(2)}) copy-start(f32[1,512,896]{2,1,0:T(8,128)} %param.17) | copy-start | bytes 5505028
  164.6 5.0 %copy-start.28 = (f32[1,512,896]{2,1,0:T(8,128)S(1)}, f32[1,512,896]{2,1,0:T(8,128)}, u32[]{:S(2)}) copy-start(f32[1,512,896]{2,1,0:T(8,128)} %param.19) | copy-start | bytes 5505028

commit v3 on v2

--- a/solution.py
+++ b/solution.py
@@ -33,14 +33,16 @@
 
 
 KEEP = 1.0 - learn_rate * weight_decay
-FIRST = learn_rate / (1.0 - beta_one**STEP)
-SECOND = 1.0 / (1.0 - beta_two**STEP)
+ROOT = ((1.0 - beta_two) / (1.0 - beta_two**STEP)) ** 0.5
+PULL = learn_rate / (1.0 - beta_one**STEP) * beta_one / ROOT
+PUSH = learn_rate / (1.0 - beta_one**STEP) * (1.0 - beta_one) / ROOT
+SPREAD = beta_two / (1.0 - beta_two)
+EDGE = adam_eps / ROOT
 
 
 def shard_of(kept, pull, spread, scaled):
-    step = pull + (FIRST * (1.0 - beta_one)) * scaled
-    width = jnp.sqrt(spread + (SECOND * (1.0 - beta_two)) * (scaled * scaled)) + adam_eps
-    return kept - step / width
+    square = spread + scaled * scaled
+    return kept - (pull + PUSH * scaled) / (square * lax.rsqrt(square) + EDGE)
 
 
 class Layout:
@@ -164,8 +166,8 @@
 
 def ready_body(master, moment, second, kept, pull, spread):
     kept[...] = KEEP * master[...]
-    pull[...] = (FIRST * beta_one) * moment[...]
-    spread[...] = (SECOND * beta_two) * second[...]
+    pull[...] = PULL * moment[...]
+    spread[...] = SPREAD * second[...]
 
 
 def ready(lay, state):
@@ -290,7 +292,7 @@
 def update_body(entries, sums, short, long, master, moment, second, shard_out, first_out, variance_out):
     scaled = clip_of(entries, sums) * jnp.where(pl.program_id(0) < HEAD, short[...], long[...])
     shard_out[...] = shard_of(
-        KEEP * master[...], (FIRST * beta_one) * moment[...], (SECOND * beta_two) * second[...], scaled
+        KEEP * master[...], PULL * moment[...], SPREAD * second[...], scaled
     )
     first_out[...] = beta_one * moment[...] + (1.0 - beta_one) * scaled
     variance_out[...] = beta_two * second[...] + (1.0 - beta_two) * (scaled * scaled)

time: 184 us -> 183 us (level)
  no operation moved by 1% of the time
where the time goes in v3:
time: 183 us
  waiting for transfers between devices  93.2 us (51%)
  Pallas kernels  34.2 us (19%)
  starting transfers between devices  32.2 us (18%)
  local copies, waits for them, and re-layouts  22 us (12%)
    ppermute x20, waiting for transfers between devices, exchange(): return lax.ppermute(value, 'dp', [(i, i ^ partner) for i in range(parts)])  93.2 us
    ppermute x20, starting transfers between devices, exchange(): return lax.ppermute(value, 'dp', [(i, i ^ partner) for i in range(parts)])  27.3 us
    unnamed x70, local copies, waits for them, and re-layouts  22 us
    pallas_call x2, Pallas kernels, update(): call(functools.partial(update_body, entries), BLOCKS, [pl.BlockSpec(sums....  7.29 us
    pallas_call x4, Pallas kernels, place_whole(): call(place_whole_body, BLOCKS, ([] if first else [pl.BlockSpec(memory_spa...  5.93 us
    all_to_all x1, starting transfers between devices, on_square(): sums = lax.all_to_all(sums, ('dp', 'mp'), 0, 0, tiled=True)  4.92 us
    pallas_call x3, Pallas kernels, cut(): pl.pallas_call(functools.partial(cut_body, lays, partners, start, blocks)...  4.02 us
  transfers between devices with their start and end apart: 21, of which 9 were waited for; matrix products, arithmetic and copies ran while one was open for 0% of the time, Pallas kernels for 17%

profile of v3, /device:TPU:0, one launch (start us, length us, event | category | flops | bytes accessed | tf_op | source)
XLA Modules:
  0.0 182.6 jit_solution(15594421945528604791)
XLA Ops:
  0.6 1.3 cut.5
  2.0 3.0 %collective-permute-start.2 = (bf16[672,512]{1,0:T(8,128)(2,1)S(1)}, bf16[672,512]{1,0:T(8,128)(2,1)S(1)}, u32[]{:S(2)}, u32[]{:S(2)}) collective-permute-start(bf16[672,512]{1,0:T(8,128)(2,1)S(1)} %get-tuple-element.43), channel_id=1, source_target_pairs={{0,8},{8,0},{16,24},{24,16},{1,9},{9,1},{17,25},{25,17},{2,10},{10... | collective-permute-start | bytes 2064392 | tf_op jit(solution)/shard_map/ppermute | solution.py:389
  5.0 1.5 collective-permute-start.6
  6.5 1.1 cut.4
  8.2 1.6 cut.3
  9.8 1.6 collective-permute-start
  11.9 14.3 %collective-permute-done.1.arrived_short = bf16[224,512]{1,0:T(8,128)(2,1)S(1)} collective-permute-done((bf16[224,512]{1,0:T(8,128)(2,1)S(1)}, bf16[224,512]{1,0:T(8,128)(2,1)S(1)}, u32[]{:S(2)}, u32[]{:S(2)}) %collective-permute-start.1) | collective-permute-done | bytes 229408 | tf_op jit(solution)/shard_map/ppermute | solution.py:389
  26.2 2.0 %collective-permute-start.5 = (bf16[128,896]{1,0:T(8,128)(2,1)S(1)}, bf16[128,896]{1,0:T(8,128)(2,1)S(1)}, u32[]{:S(2)}, u32[]{:S(2)}) collective-permute-start(bf16[128,896]{1,0:T(8,128)(2,1)S(1)} %get-tuple-element.46), channel_id=1, source_target_pairs={{0,16},{8,24},{16,0},{24,8},{1,17},{9,25},{17,1},{25,9},{2,18},{10... | collective-permute-start | bytes 688136 | tf_op jit(solution)/shard_map/ppermute | solution.py:389
  29.0 18.9 %collective-permute-done.5.arrived_short = bf16[128,896]{1,0:T(8,128)(2,1)S(1)} collective-permute-done((bf16[128,896]{1,0:T(8,128)(2,1)S(1)}, bf16[128,896]{1,0:T(8,128)(2,1)S(1)}, u32[]{:S(2)}, u32[]{:S(2)}) %collective-permute-start.5) | collective-permute-done | bytes 229408 | tf_op jit(solution)/shard_map/ppermute | solution.py:389
  47.9 0.8 shard_map.164
  48.8 2.0 %collective-permute-start.3 = (bf16[224,512]{1,0:T(8,128)(2,1)S(1)}, bf16[224,512]{1,0:T(8,128)(2,1)S(1)}, u32[]{:S(2)}, u32[]{:S(2)}) collective-permute-start(bf16[224,512]{1,0:T(8,128)(2,1)S(1)} %get-tuple-element.44), channel_id=1, source_target_pairs={{0,16},{8,24},{16,0},{24,8},{1,17},{9,25},{17,1},{25,9},{2,18},{10... | collective-permute-start | bytes 688136 | tf_op jit(solution)/shard_map/ppermute | solution.py:389
  50.8 1.5 collective-permute-start.7
  52.7 1.2 copy-done.34
  54.3 8.4 %collective-permute-done.8.arrived = bf16[672,512]{1,0:T(8,128)(2,1)S(1)} collective-permute-done((bf16[672,512]{1,0:T(8,128)(2,1)S(1)}, bf16[672,512]{1,0:T(8,128)(2,1)S(1)}, u32[]{:S(2)}, u32[]{:S(2)}) %collective-permute-start.8) | collective-permute-done | bytes 688160 | tf_op jit(solution)/shard_map/ppermute | solution.py:389
  62.9 3.0 %collective-permute-done.9.arrived = bf16[384,896]{1,0:T(8,128)(2,1)S(1)} collective-permute-done((bf16[384,896]{1,0:T(8,128)(2,1)S(1)}, bf16[384,896]{1,0:T(8,128)(2,1)S(1)}, u32[]{:S(2)}, u32[]{:S(2)}) %collective-permute-start.9) | collective-permute-done | bytes 688160 | tf_op jit(solution)/shard_map/ppermute | solution.py:389
  66.1 1.1 copy-done.14
  67.2 1.1 collective-permute-done.7.arrived_two
  68.3 0.8 shard_map.167
  69.1 0.8 copy-done.29
  69.9 0.8 copy-done.31
  70.6 4.9 %all-to-all-start = ((f32[32,1,128]{2,1,0:T(1,128)}), f32[32,1,128]{2,1,0:T(1,128)S(1)}, u32[]{:S(2)}, u32[]{:S(2)}) async-start(f32[32,1,128]{2,1,0:T(1,128)} %bitcast.5), calls=%async_computation | async-start | bytes 32768 | tf_op jit(solution)/shard_map/all_to_all | solution.py:416
  75.6 1.5 copy-done.23
  77.1 1.5 copy-done.25
  78.6 1.5 copy-done.27
  80.6 1.2 copy-done.2
  81.8 1.2 copy-done.5
  83.0 1.0 copy-done.21
  84.5 1.2 copy-done.8
  85.7 1.2 copy-done.10
  87.0 1.2 copy-done.12
  88.2 1.5 copy-done.3
  89.7 1.5 copy-done.6
  91.2 1.3 copy-done.15
  92.5 1.1 shard_map.179
  93.6 1.8 %collective-permute-start.15 = (bf16[384,896]{1,0:T(8,128)(2,1)S(1)}, bf16[384,896]{1,0:T(8,128)(2,1)S(1)}, u32[]{:S(2)}, u32[]{:S(2)}) collective-permute-start(bf16[384,896]{1,0:T(8,128)(2,1)S(1)} %shard_map.179), channel_id=1, source_target_pairs={{0,16},{8,24},{16,0},{24,8},{1,17},{9,25},{17,1},{25,9},{2,18},{10... | collective-permute-start | bytes 2064392 | tf_op jit(solution)/shard_map/ppermute | solution.py:389
  95.5 1.1 shard_map.173
  96.6 1.5 collective-permute-start.11
  98.1 1.6 shard_map.177.refs_0_
  99.8 1.0 collective-permute-start.16
  100.7 1.6 shard_map.169.refs_0_
  102.3 1.5 collective-permute-start.12
  103.8 8.2 %collective-permute-done.15.long = bf16[384,896]{1,0:T(8,128)(2,1)S(1)} collective-permute-done((bf16[384,896]{1,0:T(8,128)(2,1)S(1)}, bf16[384,896]{1,0:T(8,128)(2,1)S(1)}, u32[]{:S(2)}, u32[]{:S(2)}) %collective-permute-start.15) | collective-permute-done | bytes 688160 | tf_op jit(solution)/shard_map/ppermute | solution.py:389
  112.0 1.8 collective-permute-start.17
  113.8 1.2 collective-permute-done.11.long
  115.0 1.4 collective-permute-start.13
  117.0 0.7 collective-permute-start.14
  117.7 32.9 %collective-permute-done.14.short = bf16[128,896]{1,0:T(8,128)(2,1)S(1)} collective-permute-done((bf16[128,896]{1,0:T(8,128)(2,1)S(1)}, bf16[128,896]{1,0:T(8,128)(2,1)S(1)}, u32[]{:S(2)}, u32[]{:S(2)}) %collective-permute-start.14) | collective-permute-done | bytes 229408 | tf_op jit(solution)/shard_map/ppermute | solution.py:389
  150.6 1.6 collective-permute-start.10
  152.2 5.3 %collective-permute-done.10.short = bf16[224,512]{1,0:T(8,128)(2,1)S(1)} collective-permute-done((bf16[224,512]{1,0:T(8,128)(2,1)S(1)}, bf16[224,512]{1,0:T(8,128)(2,1)S(1)}, u32[]{:S(2)}, u32[]{:S(2)}) %collective-permute-start.10) | collective-permute-done | bytes 229408 | tf_op jit(solution)/shard_map/ppermute | solution.py:389
  157.5 1.5 collective-permute-start.18
  159.0 1.5 collective-permute-start.19
  160.5 1.5 shard_map.178._
  162.0 1.5 shard_map.170._
  163.7 0.7 copy-done.20
  164.4 3.7 %shard_map.183 = (f32[896,512]{1,0:T(8,128)}, f32[896,512]{1,0:T(8,128)}, f32[896,512]{1,0:T(8,128)}) custom-call(f32[32,128]{1,0:T(8,128)S(1)} %bitcast.51, f32[224,512]{1,0:T(8,128)S(1)} %copy-done.32, f32[672,512]{1,0:T(8,128)S(1)} %get-tuple-element.55.long.total, f32[896,512]{1,0:T(8,128)S(1)} %bitcast.33, f32[896,512]{1,0:T(8,128)S(1)} %bitcast.35, ...), custom_call_target="tpu_custom_call" | custom-call | flops 25690112 | bytes 12845056 | tf_op jit(solution)/shard_map/pallas_call | solution.py:302
  168.1 0.8 copy-done.26
  169.4 3.6 %shard_map.184 = (f32[512,896]{1,0:T(8,128)}, f32[512,896]{1,0:T(8,128)}, f32[512,896]{1,0:T(8,128)}) custom-call(f32[32,128]{1,0:T(8,128)S(1)} %bitcast.52, f32[128,896]{1,0:T(8,128)S(1)} %copy-done.30, f32[384,896]{1,0:T(8,128)S(1)} %copy-done.16, f32[512,896]{1,0:T(8,128)S(1)} %bitcast.39, f32[512,896]{1,0:T(8,128)S(1)} %bitcast.41, f32[512,896]{1,0:T(8,128)S(1)} %bitcast.43), custom_call_target="tpu_custom_call" | custom-call | flops 25690112 | bytes 12845056 | tf_op jit(solution)/shard_map/pallas_call | solution.py:302
  173.0 1.5 shard_map.180.refs_0_
  174.5 1.5 shard_map.174.refs_0_
  176.0 1.5 shard_map.181._
  177.5 1.5 shard_map.175._
  179.0 1.4 shard_map.182.__
  180.4 1.4 shard_map.176._
  181.8 0.8 place_heads.1
  (76 shorter events, 5.7 us)
Async XLA Ops:
  2.0 26.3 %collective-permute-start.2 = (bf16[672,512]{1,0:T(8,128)(2,1)S(1)}, bf16[672,512]{1,0:T(8,128)(2,1)S(1)}, u32[]{:S(2)}, u32[]{:S(2)}) collective-permute-start(bf16[672,512]{1,0:T(8,128)(2,1)S(1)} %get-tuple-element.43), channel_id=1, source_target_pairs={{0,8},{8,0},{16,24},{24,16},{1,9},{9,1},{17,25},{25,17},{2,10},{10... | collective-permute-start | bytes 2064392 | tf_op jit(solution)/shard_map/ppermute | solution.py:389
  5.0 42.9 %collective-permute-start.6 = (bf16[384,896]{1,0:T(8,128)(2,1)S(1)}, bf16[384,896]{1,0:T(8,128)(2,1)S(1)}, u32[]{:S(2)}, u32[]{:S(2)}) collective-permute-start(bf16[384,896]{1,0:T(8,128)(2,1)S(1)} %get-tuple-element.47), channel_id=1, source_target_pairs={{0,16},{8,24},{16,0},{24,8},{1,17},{9,25},{17,1},{25,9},{2,18},{10... | collective-permute-start | bytes 2064392 | tf_op jit(solution)/shard_map/ppermute | solution.py:389
  7.6 18.6 %collective-permute-start.1 = (bf16[224,512]{1,0:T(8,128)(2,1)S(1)}, bf16[224,512]{1,0:T(8,128)(2,1)S(1)}, u32[]{:S(2)}, u32[]{:S(2)}) collective-permute-start(bf16[224,512]{1,0:T(8,128)(2,1)S(1)} %get-tuple-element.42), channel_id=1, source_target_pairs={{0,8},{8,0},{16,24},{24,16},{1,9},{9,1},{17,25},{25,17},{2,10},{10... | collective-permute-start | bytes 688136 | tf_op jit(solution)/shard_map/ppermute | solution.py:389
  8.2 20.1 %copy-start = (bf16[1,1,3584,512]{3,2,1,0:T(8,128)(2,1)S(1)}, bf16[1,1,3584,512]{3,2,1,0:T(8,128)(2,1)}, u32[]{:S(2)}) copy-start(bf16[1,1,3584,512]{3,2,1,0:T(8,128)(2,1)} %param.10) | copy-start | bytes 11010052
  9.8 41.0 %collective-permute-start = (bf16[896,512]{1,0:T(8,128)(2,1)S(1)}, bf16[896,512]{1,0:T(8,128)(2,1)S(1)}, u32[]{:S(2)}, u32[]{:S(2)}) collective-permute-start(bf16[896,512]{1,0:T(8,128)(2,1)S(1)} %get-tuple-element.41), channel_id=1, source_target_pairs={{0,8},{8,0},{16,24},{24,16},{1,9},{9,1},{17,25},{25,17},{2,10},{10... | collective-permute-start | bytes 2752520 | tf_op jit(solution)/shard_map/ppermute | solution.py:389
  11.4 41.3 %collective-permute-start.4 = (bf16[512,896]{1,0:T(8,128)(2,1)S(1)}, bf16[512,896]{1,0:T(8,128)(2,1)S(1)}, u32[]{:S(2)}, u32[]{:S(2)}) collective-permute-start(bf16[512,896]{1,0:T(8,128)(2,1)S(1)} %get-tuple-element.45), channel_id=1, source_target_pairs={{0,16},{8,24},{16,0},{24,8},{1,17},{9,25},{17,1},{25,9},{2,18},{10... | collective-permute-start | bytes 2752520 | tf_op jit(solution)/shard_map/ppermute | solution.py:389
  26.2 21.7 %copy-start.1 = (bf16[1,1,512,3584]{3,2,1,0:T(8,128)(2,1)S(1)}, bf16[1,1,512,3584]{3,2,1,0:T(8,128)(2,1)}, u32[]{:S(2)}) copy-start(bf16[1,1,512,3584]{3,2,1,0:T(8,128)(2,1)} %param.11) | copy-start | bytes 11010052
  26.2 21.7 %collective-permute-start.5 = (bf16[128,896]{1,0:T(8,128)(2,1)S(1)}, bf16[128,896]{1,0:T(8,128)(2,1)S(1)}, u32[]{:S(2)}, u32[]{:S(2)}) collective-permute-start(bf16[128,896]{1,0:T(8,128)(2,1)S(1)} %get-tuple-element.46), channel_id=1, source_target_pairs={{0,16},{8,24},{16,0},{24,8},{1,17},{9,25},{17,1},{25,9},{2,18},{10... | collective-permute-start | bytes 688136 | tf_op jit(solution)/shard_map/ppermute | solution.py:389
  28.9 23.4 %copy-start.33 = (f32[1,896,512]{2,1,0:T(8,128)S(1)}, f32[1,896,512]{2,1,0:T(8,128)}, u32[]{:S(2)}) copy-start(f32[1,896,512]{2,1,0:T(8,128)} %param.12) | copy-start | bytes 5505028
  28.9 33.8 %collective-permute-start.8 = (bf16[672,512]{1,0:T(8,128)(2,1)S(1)}, bf16[672,512]{1,0:T(8,128)(2,1)S(1)}, u32[]{:S(2)}, u32[]{:S(2)}) collective-permute-start(bf16[672,512]{1,0:T(8,128)(2,1)S(1)} %get-tuple-element.49), channel_id=1, source_target_pairs={{0,16},{8,24},{16,0},{24,8},{1,17},{9,25},{17,1},{25,9},{2,18},{10... | collective-permute-start | bytes 2064392 | tf_op jit(solution)/shard_map/ppermute | solution.py:389
  48.7 17.2 %collective-permute-start.9 = (bf16[384,896]{1,0:T(8,128)(2,1)S(1)}, bf16[384,896]{1,0:T(8,128)(2,1)S(1)}, u32[]{:S(2)}, u32[]{:S(2)}) collective-permute-start(bf16[384,896]{1,0:T(8,128)(2,1)S(1)} %get-tuple-element.51), channel_id=1, source_target_pairs={{0,8},{8,0},{16,24},{24,16},{1,9},{9,1},{17,25},{25,17},{2,10},{10... | collective-permute-start | bytes 2064392 | tf_op jit(solution)/shard_map/ppermute | solution.py:389
  48.8 18.4 %collective-permute-start.3 = (bf16[224,512]{1,0:T(8,128)(2,1)S(1)}, bf16[224,512]{1,0:T(8,128)(2,1)S(1)}, u32[]{:S(2)}, u32[]{:S(2)}) collective-permute-start(bf16[224,512]{1,0:T(8,128)(2,1)S(1)} %get-tuple-element.44), channel_id=1, source_target_pairs={{0,16},{8,24},{16,0},{24,8},{1,17},{9,25},{17,1},{25,9},{2,18},{10... | collective-permute-start | bytes 688136 | tf_op jit(solution)/shard_map/ppermute | solution.py:389
  50.8 17.5 %collective-permute-start.7 = (bf16[128,896]{1,0:T(8,128)(2,1)S(1)}, bf16[128,896]{1,0:T(8,128)(2,1)S(1)}, u32[]{:S(2)}, u32[]{:S(2)}) collective-permute-start(bf16[128,896]{1,0:T(8,128)(2,1)S(1)} %get-tuple-element.48), channel_id=1, source_target_pairs={{0,8},{8,0},{16,24},{24,16},{1,9},{9,1},{17,25},{25,17},{2,10},{10... | collective-permute-start | bytes 688136 | tf_op jit(solution)/shard_map/ppermute | solution.py:389
  52.3 1.5 copy-start.34
  66.1 1.1 copy-start.14
  69.1 0.8 copy-start.29
  69.9 0.8 copy-start.31
  70.6 17.5 %all-to-all-start = ((f32[32,1,128]{2,1,0:T(1,128)}), f32[32,1,128]{2,1,0:T(1,128)S(1)}, u32[]{:S(2)}, u32[]{:S(2)}) async-start(f32[32,1,128]{2,1,0:T(1,128)} %bitcast.5), calls=%async_computation | async-start | bytes 32768 | tf_op jit(solution)/shard_map/all_to_all | solution.py:416
  75.6 1.5 copy-start.23
  77.1 1.5 copy-start.25
  78.6 1.5 copy-start.27
  80.1 3.0 %copy-start.17 = (f32[1,896,512]{2,1,0:T(8,128)S(1)}, f32[1,896,512]{2,1,0:T(8,128)}, u32[]{:S(2)}) copy-start(f32[1,896,512]{2,1,0:T(8,128)} %param.14) | copy-start | bytes 5505028
  80.1 3.0 %copy-start.19 = (f32[1,896,512]{2,1,0:T(8,128)S(1)}, f32[1,896,512]{2,1,0:T(8,128)}, u32[]{:S(2)}) copy-start(f32[1,896,512]{2,1,0:T(8,128)} %param.16) | copy-start | bytes 5505028
  80.1 3.9 %copy-start.21 = (f32[1,896,512]{2,1,0:T(8,128)S(1)}, f32[1,896,512]{2,1,0:T(8,128)}, u32[]{:S(2)}) copy-start(f32[1,896,512]{2,1,0:T(8,128)} %param.18) | copy-start | bytes 5505028
  80.6 1.2 copy-start.2
  81.8 1.2 copy-start.5
  84.5 1.2 copy-start.8
  85.7 1.2 copy-start.10
  87.0 1.2 copy-start.12
  88.2 1.5 copy-start.3
  89.7 1.5 copy-start.6
  91.2 1.3 copy-start.15
  92.5 2.9 %copy-start.9 = (f32[896,512]{1,0:T(8,128)S(1)}, f32[896,512]{1,0:T(8,128)}, u32[]{:S(2)}) copy-start(f32[896,512]{1,0:T(8,128)} %copy-done.8) | copy-start | bytes 5505028
  92.5 2.9 %copy-start.11 = (f32[896,512]{1,0:T(8,128)S(1)}, f32[896,512]{1,0:T(8,128)}, u32[]{:S(2)}) copy-start(f32[896,512]{1,0:T(8,128)} %copy-done.10) | copy-start | bytes 5505028
  92.5 2.9 %copy-start.13 = (f32[896,512]{1,0:T(8,128)S(1)}, f32[896,512]{1,0:T(8,128)}, u32[]{:S(2)}) copy-start(f32[896,512]{1,0:T(8,128)} %copy-done.12) | copy-start | bytes 5505028
  93.6 18.4 %collective-permute-start.15 = (bf16[384,896]{1,0:T(8,128)(2,1)S(1)}, bf16[384,896]{1,0:T(8,128)(2,1)S(1)}, u32[]{:S(2)}, u32[]{:S(2)}) collective-permute-start(bf16[384,896]{1,0:T(8,128)(2,1)S(1)} %shard_map.179), channel_id=1, source_target_pairs={{0,16},{8,24},{16,0},{24,8},{1,17},{9,25},{17,1},{25,9},{2,18},{10... | collective-permute-start | bytes 2064392 | tf_op jit(solution)/shard_map/ppermute | solution.py:389
  95.5 2.7 %copy-start.4 = (f32[512,896]{1,0:T(8,128)S(1)}, f32[512,896]{1,0:T(8,128)}, u32[]{:S(2)}) copy-start(f32[512,896]{1,0:T(8,128)} %copy-done.2) | copy-start | bytes 5505028
  95.5 2.7 %copy-start.7 = (f32[512,896]{1,0:T(8,128)S(1)}, f32[512,896]{1,0:T(8,128)}, u32[]{:S(2)}) copy-start(f32[512,896]{1,0:T(8,128)} %copy-done.5) | copy-start | bytes 5505028
  95.5 2.6 %copy-start.30 = (f32[128,896]{1,0:T(8,128)S(1)}, f32[128,896]{1,0:T(8,128)}, u32[]{:S(2)}) copy-start(f32[128,896]{1,0:T(8,128)} %copy-done.29) | copy-start | bytes 1376260
  96.6 18.4 %collective-permute-start.11 = (bf16[672,512]{1,0:T(8,128)(2,1)S(1)}, bf16[672,512]{1,0:T(8,128)(2,1)S(1)}, u32[]{:S(2)}, u32[]{:S(2)}) collective-permute-start(bf16[672,512]{1,0:T(8,128)(2,1)S(1)} %shard_map.173), channel_id=1, source_target_pairs={{0,8},{8,0},{16,24},{24,16},{1,9},{9,1},{17,25},{25,17},{2,10},{10... | collective-permute-start | bytes 2064392 | tf_op jit(solution)/shard_map/ppermute | solution.py:389
  98.1 2.6 %copy-start.32 = (f32[224,512]{1,0:T(8,128)S(1)}, f32[224,512]{1,0:T(8,128)}, u32[]{:S(2)}) copy-start(f32[224,512]{1,0:T(8,128)} %copy-done.31) | copy-start | bytes 1376260
  99.8 59.3 %collective-permute-start.16 = (bf16[512,896]{1,0:T(8,128)(2,1)S(1)}, bf16[512,896]{1,0:T(8,128)(2,1)S(1)}, u32[]{:S(2)}, u32[]{:S(2)}) collective-permute-start(bf16[512,896]{1,0:T(8,128)(2,1)S(1)} %shard_map.177.refs_0_), channel_id=1, source_target_pairs={{0,8},{8,0},{16,24},{24,16},{1,9},{9,1},{17,25},{25,17},{2,10},{10... | collective-permute-start | bytes 2752520 | tf_op jit(solution)/shard_map/ppermute | solution.py:389
  102.3 75.2 %collective-permute-start.12 = (bf16[896,512]{1,0:T(8,128)(2,1)S(1)}, bf16[896,512]{1,0:T(8,128)(2,1)S(1)}, u32[]{:S(2)}, u32[]{:S(2)}) collective-permute-start(bf16[896,512]{1,0:T(8,128)(2,1)S(1)} %shard_map.169.refs_0_), channel_id=1, source_target_pairs={{0,16},{8,24},{16,0},{24,8},{1,17},{9,25},{17,1},{25,9},{2,18},{10... | collective-permute-start | bytes 2752520 | tf_op jit(solution)/shard_map/ppermute | solution.py:389
  112.0 67.0 %collective-permute-start.17 = (bf16[384,896]{1,0:T(8,128)(2,1)S(1)}, bf16[384,896]{1,0:T(8,128)(2,1)S(1)}, u32[]{:S(2)}, u32[]{:S(2)}) collective-permute-start(bf16[384,896]{1,0:T(8,128)(2,1)S(1)} %collective-permute-done.15.long), channel_id=1, source_target_pairs={{0,8},{8,0},{16,24},{24,16},{1,9},{9,1},{17,25},{25,17},{2,10},{10... | collective-permute-start | bytes 2064392 | tf_op jit(solution)/shard_map/ppermute | solution.py:389
  115.0 65.4 %collective-permute-start.13 = (bf16[672,512]{1,0:T(8,128)(2,1)S(1)}, bf16[672,512]{1,0:T(8,128)(2,1)S(1)}, u32[]{:S(2)}, u32[]{:S(2)}) collective-permute-start(bf16[672,512]{1,0:T(8,128)(2,1)S(1)} %collective-permute-done.11.long), channel_id=1, source_target_pairs={{0,16},{8,24},{16,0},{24,8},{1,17},{9,25},{17,1},{25,9},{2,18},{10... | collective-permute-start | bytes 2064392 | tf_op jit(solution)/shard_map/ppermute | solution.py:389
  117.0 33.6 %collective-permute-start.14 = (bf16[128,896]{1,0:T(8,128)(2,1)S(1)}, bf16[128,896]{1,0:T(8,128)(2,1)S(1)}, u32[]{:S(2)}, u32[]{:S(2)}) collective-permute-start(bf16[128,896]{1,0:T(8,128)(2,1)S(1)} %get-tuple-element.65), channel_id=1, source_target_pairs={{0,16},{8,24},{16,0},{24,8},{1,17},{9,25},{17,1},{25,9},{2,18},{10... | collective-permute-start | bytes 688136 | tf_op jit(solution)/shard_map/ppermute | solution.py:389
  150.6 6.9 %collective-permute-start.10 = (bf16[224,512]{1,0:T(8,128)(2,1)S(1)}, bf16[224,512]{1,0:T(8,128)(2,1)S(1)}, u32[]{:S(2)}, u32[]{:S(2)}) collective-permute-start(bf16[224,512]{1,0:T(8,128)(2,1)S(1)} %get-tuple-element.63), channel_id=1, source_target_pairs={{0,8},{8,0},{16,24},{24,16},{1,9},{9,1},{17,25},{25,17},{2,10},{10... | collective-permute-start | bytes 688136 | tf_op jit(solution)/shard_map/ppermute | solution.py:389
  157.5 24.3 %collective-permute-start.18 = (bf16[224,512]{1,0:T(8,128)(2,1)S(1)}, bf16[224,512]{1,0:T(8,128)(2,1)S(1)}, u32[]{:S(2)}, u32[]{:S(2)}) collective-permute-start(bf16[224,512]{1,0:T(8,128)(2,1)S(1)} %collective-permute-done.10.short), channel_id=1, source_target_pairs={{0,16},{8,24},{16,0},{24,8},{1,17},{9,25},{17,1},{25,9},{2,18},{10... | collective-permute-start | bytes 688136 | tf_op jit(solution)/shard_map/ppermute | solution.py:389
  159.0 22.8 %collective-permute-start.19 = (bf16[128,896]{1,0:T(8,128)(2,1)S(1)}, bf16[128,896]{1,0:T(8,128)(2,1)S(1)}, u32[]{:S(2)}, u32[]{:S(2)}) collective-permute-start(bf16[128,896]{1,0:T(8,128)(2,1)S(1)} %collective-permute-done.14.short), channel_id=1, source_target_pairs={{0,8},{8,0},{16,24},{24,16},{1,9},{9,1},{17,25},{25,17},{2,10},{10... | collective-permute-start | bytes 688136 | tf_op jit(solution)/shard_map/ppermute | solution.py:389
  160.5 3.0 %copy-start.22 = (f32[1,896,512]{2,1,0:T(8,128)S(1)}, f32[1,896,512]{2,1,0:T(8,128)}, u32[]{:S(2)}) copy-start(f32[1,896,512]{2,1,0:T(8,128)} %param.18) | copy-start | bytes 5505028
  162.0 1.7 copy-start.18
  162.0 2.4 %copy-start.20 = (f32[1,896,512]{2,1,0:T(8,128)S(1)}, f32[1,896,512]{2,1,0:T(8,128)}, u32[]{:S(2)}) copy-start(f32[1,896,512]{2,1,0:T(8,128)} %param.16) | copy-start | bytes 5505028
  164.4 3.7 %copy-start.16 = (f32[384,896]{1,0:T(8,128)S(1)}, f32[384,896]{1,0:T(8,128)}, u32[]{:S(2)}) copy-start(f32[384,896]{1,0:T(8,128)} %copy-done.14) | copy-start | bytes 4128772
  164.4 3.7 %copy-start.24 = (f32[1,512,896]{2,1,0:T(8,128)S(1)}, f32[1,512,896]{2,1,0:T(8,128)}, u32[]{:S(2)}) copy-start(f32[1,512,896]{2,1,0:T(8,128)} %param.15) | copy-start | bytes 5505028
  164.4 4.4 %copy-start.26 = (f32[1,512,896]{2,1,0:T(8,128)S(1)}, f32[1,512,896]{2,1,0:T(8,128)}, u32[]{:S(2)}) copy-start(f32[1,512,896]{2,1,0:T(8,128)} %param.17) | copy-start | bytes 5505028
  164.4 5.0 %copy-start.28 = (f32[1,512,896]{2,1,0:T(8,128)S(1)}, f32[1,512,896]{2,1,0:T(8,128)}, u32[]{:S(2)}) copy-start(f32[1,512,896]{2,1,0:T(8,128)} %param.19) | copy-start | bytes 5505028
